TPU v7x, 128 devices: a whole 4x4x4 slice. The times are simulated.
128 devices in a mesh: rows: 8 (over x, core), cols: 16 (over y, z).
Axes of the slice: x: 4, y: 4, z: 4, core: 2. Of those that a mesh axis runs over, the one named last changes fastest.
Arguments:
- slab: float32 [65536, 2048], P('rows', 'cols'), may hold values from -6 to 6
- sign_bits: int32 [65536], P('rows'), may hold values from 0 to 1
- sample_rows: int32 [8192], replicated, may hold values from 0 to 65535, as said below
Outputs:
- gram: float32 [2048, 2048], P('rows', 'cols')
Inputs may be any that keep to these rules, and one draw needn't show every extreme that they name: `sample_rows`: Ascending; repeats may occur. At most 2048 indices fall in any one device's aligned block of 8192 rows, and some block holds exactly 2048.
All inputs are finite; a program needn't handle non-finite values.
Results may differ from a plain program's by a relative error of at most 0.000071.
Values sent between devices are 32-bit elements; how exact they have to be, the bound alone decides.
A program may use at most 64 MiB of HBM per device.

v0:
```python
import jax
import jax.numpy as jnp
from jax import lax
from jax.sharding import PartitionSpec as P

CAP = 2048


def from_partner(shard, axis, bit):
    return lax.ppermute(shard, axis, [(i, i ^ 1 << bit) for i in range(lax.axis_size(axis))])


def parity_table(length):
    index_list = jnp.arange(length, dtype=jnp.int32)
    common = index_list[:, None] & index_list[None, :]
    parity = jnp.zeros((length, length), jnp.int32)
    for bit_number in range(max(length.bit_length() - 1, 0)):
        parity = parity + (common >> bit_number & 1)
    return (1 - 2 * (parity % 2)).astype(jnp.float32)


def local_transform(slab, sign_bits):
    height, columns = slab.shape
    flipped = slab * (1 - 2 * sign_bits).astype(jnp.float32)[:, None]
    blocks = flipped.reshape(height // 128, 128, columns)
    inside = jnp.einsum("ij,qjc->qic", parity_table(128), blocks, precision=lax.Precision.HIGHEST)
    outside = jnp.einsum(
        "pq,qic->pic", parity_table(height // 128), inside, precision=lax.Precision.HIGHEST
    )
    return outside.reshape(height, columns)


def column_product(portion, own_rows):
    return lax.dot_general(
        portion,
        own_rows,
        (((0,), (0,)), ((), ())),
        precision=lax.Precision.HIGHEST,
        preferred_element_type=jnp.float32,
    )


def shards(slab, sign_bits, sample_rows):
    mixed_rows = local_transform(slab, sign_bits)
    height = mixed_rows.shape[0]
    groups = lax.axis_size("rows")
    my_index = lax.axis_index("rows")
    samples = sample_rows.shape[0]
    factor = 1.0 / (samples * height * groups)
    for bit_number in range(groups.bit_length() - 1):
        partner = from_partner(mixed_rows, "rows", bit_number)
        is_upper = my_index >> bit_number & 1 == 1
        mixed_rows = jnp.where(is_upper, partner - mixed_rows, mixed_rows + partner)
    lowest = my_index * height
    first_slot = jnp.sum((sample_rows < lowest).astype(jnp.int32))
    length = jnp.sum(((sample_rows >= lowest) & (sample_rows < lowest + height)).astype(jnp.int32))
    padded = jnp.concatenate([sample_rows, jnp.zeros((CAP,), jnp.int32)])
    window = lax.dynamic_slice_in_dim(padded, first_slot, CAP)
    offsets = jnp.clip(window - lowest, 0, height - 1)
    picked = jnp.take(mixed_rows, offsets, axis=0)
    picked = jnp.where((jnp.arange(CAP, dtype=jnp.int32) < length)[:, None], picked, 0.0)
    terms = column_product(lax.all_gather(picked, "cols", axis=1, tiled=True), picked)
    return lax.psum_scatter(terms * factor, "rows", scatter_dimension=0, tiled=True)


def solution(mesh):
    return jax.shard_map(
        shards,
        mesh=mesh,
        in_specs=(P("rows", "cols"), P("rows"), P()),
        out_specs=P("rows", "cols"),
        check_vma=False,
    )
```

profile of v0, /device:TPU:1, one launch (start us, length us, event | category | flops | bytes accessed | tf_op | source)
XLA Modules:
  0.0 446.6 jit_solution(5406967571214088147)
XLA Ops:
  6.5 0.0 all-gather.2.cloned.1.call-start
  6.5 0.8 subtract_convert_fusion
  7.3 5.0 %broadcast_multiply_fusion = f32[8192,128]{1,0:T(8,128)S(1)} fusion(f32[8192,128]{1,0:T(8,128)} %param.3, f32[8192]{0:T(1024)S(1)} %subtract_convert_fusion), kind=kLoop, calls=%fused_computation.7 | loop fusion | flops 1048576 | bytes 8421376 | tf_op jit(solution)/shard_map/mul | solution.py:24
  12.3 8.4 %fusion.7 = f32[64,128,128]{2,1,0:T(8,128)} fusion(f32[64,128,128]{2,1,0:T(8,128)S(1)} %bitcast.15), kind=kOutput, calls=%fused_computation.17 | convolution fusion | flops 1611186176 | bytes 8388608 | tf_op jit(solution)/shard_map/ij,qjc->qic/dot_general | solution.py:26
  20.6 5.4 %copy.5 = f32[64,128,128]{1,0,2:T(8,128)} copy(f32[64,128,128]{2,1,0:T(8,128)} %fusion.7) | data formatting | bytes 8388608 | tf_op jit(solution)/shard_map/ij,qjc->qic/dot_general | solution.py:26
  26.0 5.5 %fusion = f32[64,128,128]{2,0,1:T(8,128)S(1)} fusion(f32[64,128,128]{1,0,2:T(8,128)} %copy.5), kind=kOutput, calls=%fused_computation.1 | convolution fusion | flops 805437440 | bytes 8388608 | tf_op jit(solution)/shard_map/pq,qic->pic/dot_general | solution.py:27
  31.6 4.4 copy.4
  35.9 1.4 collective-permute-start
  37.3 7.1 %collective-permute-done = f32[8192,128]{1,0:T(8,128)} collective-permute-done((f32[8192,128]{1,0:T(8,128)}, f32[8192,128]{1,0:T(8,128)}, u32[]{:S(2)}, u32[]{:S(2)}) %collective-permute-start) | collective-permute-done | bytes 4194336 | tf_op jit(solution)/shard_map/ppermute | solution.py:10
  44.4 5.9 %add_select_fusion.2 = f32[8192,128]{1,0:T(8,128)} fusion(f32[8192,128]{1,0:T(8,128)} %collective-permute-done, pred[]{:T(512)S(6)} %eq.15, f32[64,128,128]{2,1,0:T(8,128)} %copy.4), kind=kLoop, calls=%fused_computation.5 | loop fusion | flops 3145728 | bytes 12582913 | tf_op jit(solution)/shard_map/jit(_where)/select_n | solution.py:53
  50.3 1.3 collective-permute-start.1
  51.6 0.0 copy-start
  51.6 90.7 %collective-permute-done.1 = f32[8192,128]{1,0:T(8,128)} collective-permute-done((f32[8192,128]{1,0:T(8,128)}, f32[8192,128]{1,0:T(8,128)}, u32[]{:S(2)}, u32[]{:S(2)}) %collective-permute-start.1) | collective-permute-done | bytes 4194336 | tf_op jit(solution)/shard_map/ppermute | solution.py:10
  142.4 5.9 %add_select_fusion.1 = f32[8192,128]{1,0:T(8,128)} fusion(f32[8192,128]{1,0:T(8,128)} %add_select_fusion.2, f32[8192,128]{1,0:T(8,128)} %collective-permute-done.1, pred[]{:T(512)S(6)} %eq.14), kind=kLoop, calls=%fused_computation.4 | loop fusion | flops 3145728 | bytes 12582913 | tf_op jit(solution)/shard_map/jit(_where)/select_n | solution.py:53
  148.3 2.9 collective-permute-start.2
  151.1 0.0 copy-done
  151.1 0.6 convert_reduce_fusion.1
  153.4 0.7 iota_compare_fusion
  154.1 0.1 broadcast_clamp_fusion
  154.2 86.7 %collective-permute-done.2 = f32[8192,128]{1,0:T(8,128)} collective-permute-done((f32[8192,128]{1,0:T(8,128)}, f32[8192,128]{1,0:T(8,128)}, u32[]{:S(2)}, u32[]{:S(2)}) %collective-permute-start.2) | collective-permute-done | bytes 4194336 | tf_op jit(solution)/shard_map/ppermute | solution.py:10
  241.0 5.9 %add_select_fusion = f32[8192,128]{1,0:T(8,128)} fusion(f32[8192,128]{1,0:T(8,128)} %add_select_fusion.1, f32[8192,128]{1,0:T(8,128)} %collective-permute-done.2, pred[]{:T(512)S(6)} %eq.13), kind=kLoop, calls=%fused_computation.3 | loop fusion | flops 3145728 | bytes 12582913 | tf_op jit(solution)/shard_map/jit(_where)/select_n | solution.py:53
  246.8 7.6 %gather_fusion = f32[2048,128]{1,0:T(8,128)S(1)} fusion(f32[8192,128]{1,0:T(8,128)} %add_select_fusion, s32[2048]{0:T(1024)S(1)} %broadcast_clamp_fusion), kind=kCustom, calls=%fused_computation | custom fusion | bytes 2105344 | tf_op jit(solution)/shard_map/jit(_take)/gather | solution.py:60
  254.5 2.4 select_select_fusion
  256.9 0.0 all-gather.2.cloned.1.call-update
  256.9 0.0 reduce-scatter.2.cloned.1.call-start
  257.0 122.6 %all-gather.2.cloned.1.call-done = f32[2048,2048]{1,0:T(8,128)} async-done(((f32[2048,128]{1,0:T(8,128)}), f32[2048,2048]{1,0:T(8,128)}) %all-gather.2.cloned.1.call-update) | async-done | bytes 16777232 | tf_op jit(solution)/shard_map/all_gather | solution.py:62
  379.6 29.9 %convolution_multiply_fusion = f32[2048,128]{1,0:T(8,128)} fusion(f32[2048,2048]{1,0:T(8,128)} %all-gather.2.cloned.1.call-done, f32[2048,128]{1,0:T(8,128)} %select_select_fusion), kind=kOutput, calls=%fused_computation.6 | convolution fusion | flops 6442713088 | bytes 18874368 | tf_op jit(solution)/shard_map/dot_general | solution.py:34
  409.5 0.0 reduce-scatter.2.cloned.1.call-update
  409.5 30.3 %reduce-scatter.2.cloned.1.call-done = f32[256,128]{1,0:T(8,128)} async-done(((f32[2048,128]{1,0:T(8,128)}), f32[256,128]{1,0:T(8,128)}) %reduce-scatter.2.cloned.1.call-update) | async-done | bytes 131088 | tf_op jit(solution)/shard_map/reduce_scatter | solution.py:63
Async XLA Ops:
  6.5 373.1 %all-gather.2.cloned.1.call-start = ((), (), s32[]{:S(2)}) async-start(), calls=%async_computation.1 | async-start | bytes 17825792 | tf_op jit(solution)/shard_map/all_gather | solution.py:62
  35.9 8.5 %collective-permute-start = (f32[8192,128]{1,0:T(8,128)}, f32[8192,128]{1,0:T(8,128)}, u32[]{:S(2)}, u32[]{:S(2)}) collective-permute-start(f32[8192,128]{1,0:T(8,128)} %bitcast.4), channel_id=1, source_target_pairs={{0,16},{16,0},{32,48},{48,32},{64,80},{80,64},{96,112},{112,96},{1... | collective-permute-start | bytes 12582920 | tf_op jit(solution)/shard_map/ppermute | solution.py:10
  50.3 92.1 %collective-permute-start.1 = (f32[8192,128]{1,0:T(8,128)}, f32[8192,128]{1,0:T(8,128)}, u32[]{:S(2)}, u32[]{:S(2)}) collective-permute-start(f32[8192,128]{1,0:T(8,128)} %add_select_fusion.2), channel_id=1, source_target_pairs={{0,32},{16,48},{32,0},{48,16},{64,96},{80,112},{96,64},{112,80},{1... | collective-permute-start | bytes 12582920 | tf_op jit(solution)/shard_map/ppermute | solution.py:10
  51.6 99.5 %copy-start = (s32[8192]{0:T(1024)S(1)}, s32[8192]{0:T(1024)}, u32[]{:S(2)}) copy-start(s32[8192]{0:T(1024)} %param.5) | copy-start | bytes 98308
  148.3 92.7 %collective-permute-start.2 = (f32[8192,128]{1,0:T(8,128)}, f32[8192,128]{1,0:T(8,128)}, u32[]{:S(2)}, u32[]{:S(2)}) collective-permute-start(f32[8192,128]{1,0:T(8,128)} %add_select_fusion.1), channel_id=1, source_target_pairs={{0,64},{16,80},{32,96},{48,112},{64,0},{80,16},{96,32},{112,48},{1... | collective-permute-start | bytes 12582920 | tf_op jit(solution)/shard_map/ppermute | solution.py:10
  256.9 182.8 %reduce-scatter.2.cloned.1.call-start = ((), (), s32[]{:S(2)}) async-start(), calls=%async_computation.2 | async-start | bytes 1179648 | tf_op jit(solution)/shard_map/reduce_scatter | solution.py:63
Sparse Core Ops, SparseCore 0:
  257.1 122.5 all-gather.1
  409.6 30.0 reduce-scatter.1
where the time goes:
time: 449 us; the launch traced here: 447 us
  waiting for transfers between devices  338 us (75%)
  matrix products  43.7 us (10%)
  other arithmetic  27.2 us (6%)
  local copies, waits for them, and re-layouts  17.4 us (4%)
  between operations  15.1 us (3%)
  starting transfers between devices  5.61 us (1%)
    ppermute x3, waiting for transfers between devices, from_partner(): lax.ppermute(shard, axis, [(i, i ^ 1 << bit) for i in range(lax.axis_size...  185 us
    all_gather x1, waiting for transfers between devices, shards(): lax.all_gather(picked, 'cols', axis=1, tiled=True)  123 us
    reduce_scatter x1, waiting for transfers between devices, shards(): lax.psum_scatter(terms * factor, 'rows', scatter_dimension=0, tiled=True)  30.3 us
    dot_general x1, matrix products, column_product(): lax.dot_general(portion, own_rows, (((0,), (0,)), ((), ())), precision=la...  29.9 us
    select_n x3, other arithmetic, shards(): mixed_rows = jnp.where(is_upper, partner - mixed_rows, mixed_rows + partner)  17.6 us
  transfers between devices with their start and end apart: 5, of which 5 were waited for; matrix products, arithmetic and copies ran while one was open for 0% of the time, Pallas kernels for 0%

commit v1 on v0

v1 whole, which is shorter than its diff:
```python
import jax
import jax.numpy as jnp
from jax import lax
from jax.sharding import PartitionSpec as P


def parity_table(length):
    index_list = jnp.arange(length, dtype=jnp.int32)
    common = index_list[:, None] & index_list[None, :]
    parity = jnp.zeros((length, length), jnp.int32)
    for bit_number in range(max(length.bit_length() - 1, 0)):
        parity = parity + (common >> bit_number & 1)
    return (1 - 2 * (parity % 2)).astype(jnp.float32)


def local_transform(slab, sign_bits):
    height, columns = slab.shape
    flipped = slab * (1 - 2 * sign_bits).astype(jnp.float32)[:, None]
    blocks = flipped.reshape(height // 128, 128, columns)
    inside = jnp.einsum("ij,qjc->qic", parity_table(128), blocks, precision=lax.Precision.HIGHEST)
    outside = jnp.einsum(
        "pq,qic->pic", parity_table(height // 128), inside, precision=lax.Precision.HIGHEST
    )
    return outside.reshape(height, columns)


def column_product(portion, own_rows):
    return lax.dot_general(
        portion,
        own_rows,
        (((0,), (0,)), ((), ())),
        precision=lax.Precision.HIGHEST,
        preferred_element_type=jnp.float32,
    )


def shards(slab, sign_bits, sample_rows):
    local = local_transform(slab, sign_bits)
    height = local.shape[0]
    groups = lax.axis_size("rows")
    me = lax.axis_index("rows")
    samples = sample_rows.shape[0]
    factor = 1.0 / (samples * height * groups)
    offsets = sample_rows % height
    common = (sample_rows // height) & me
    parity = (common ^ common >> 1 ^ common >> 2) & 1
    terms = jnp.take(local, offsets, axis=0) * (1 - 2 * parity).astype(jnp.float32)[:, None]
    picked = lax.psum_scatter(terms, "rows", scatter_dimension=0, tiled=True)
    gram = column_product(lax.all_gather(picked, "cols", axis=1, tiled=True), picked)
    return lax.psum_scatter(gram * factor, "rows", scatter_dimension=0, tiled=True)


def solution(mesh):
    return jax.shard_map(
        shards,
        mesh=mesh,
        in_specs=(P("rows", "cols"), P("rows"), P()),
        out_specs=P("rows", "cols"),
        check_vma=False,
    )
```

time: 449 us -> 252 us (0.56)
  waiting for transfers between devices: 338 us -> 148 us
  local copies, waits for them, and re-layouts: 17.4 us -> 39.8 us
  matrix products: 43.7 us -> 30.3 us
  other arithmetic: 27.2 us -> 17 us
  starting transfers between devices: 5.61 us -> 0.26 us
    ppermute x3 -> x0, waiting for transfers between devices: 185 us -> none  [from_partner(): lax.ppermute(shard, axis, [(i, i ^ 1 << bit) for i in range(lax.axis_size...]
    all_gather x1, waiting for transfers between devices: 123 us -> 79.7 us  [shards(): lax.all_gather(picked, 'cols', axis=1, tiled=True)]
    reduce_scatter x1 -> x2, waiting for transfers between devices: 30.3 us -> 68.6 us  [the longest x1 38.3 us: shards(): picked = lax.psum_scatter(terms, 'rows', scatter_dimension=0, tiled=True)]
    gather x1, local copies, waits for them, and re-layouts: 7.65 us -> 30.1 us  [shards(): jnp.take(local, offsets, axis=0)]
    select_n x4 -> x0, other arithmetic: 20 us -> none  [the longest x3 17.6 us: shards(): mixed_rows = jnp.where(is_upper, partner - mixed_rows, mixed_rows + partner)]
    dot_general x1, matrix products: 29.9 us -> 16.5 us  [column_product(): lax.dot_general(portion, own_rows, (((0,), (0,)), ((), ())), precision=la...]
    mul x0 -> x1, other arithmetic: none -> 9.71 us  [shards(): jnp.take(local, offsets, axis=0)]
    ppermute x3 -> x0, starting transfers between devices: 5.57 us -> none  [from_partner(): lax.ppermute(shard, axis, [(i, i ^ 1 << bit) for i in range(lax.axis_size...]
  transfers between devices with their start and end apart: 5 -> 3, of which waited for: 5 -> 3; matrix products, arithmetic and copies ran while one was open for 0% -> 0% of each run, Pallas kernels for 0% -> 0%
where the time goes in v1:
time: 252 us; the launch traced here: 249 us
  waiting for transfers between devices  148 us (59%)
  local copies, waits for them, and re-layouts  39.8 us (16%)
  matrix products  30.3 us (12%)
  other arithmetic  17 us (7%)
  between operations  13.1 us (5%)
    all_gather x1, waiting for transfers between devices, shards(): lax.all_gather(picked, 'cols', axis=1, tiled=True)  79.7 us
    reduce_scatter x1, waiting for transfers between devices, shards(): picked = lax.psum_scatter(terms, 'rows', scatter_dimension=0, tiled=True)  38.3 us
    reduce_scatter x1, waiting for transfers between devices, shards(): lax.psum_scatter(gram * factor, 'rows', scatter_dimension=0, tiled=True)  30.3 us
    gather x1, local copies, waits for them, and re-layouts, shards(): jnp.take(local, offsets, axis=0)  30.1 us
    dot_general x1, matrix products, column_product(): lax.dot_general(portion, own_rows, (((0,), (0,)), ((), ())), precision=la...  16.5 us
    mul x1, other arithmetic, shards(): jnp.take(local, offsets, axis=0)  9.71 us
    dot_general x1, matrix products, local_transform(): jnp.einsum('ij,qjc->qic', parity_table(128), blocks, precision=lax.Precis...  8.36 us
    dot_general x1, matrix products, local_transform(): jnp.einsum('pq,qic->pic', parity_table(height // 128), inside, precision=...  5.51 us
  transfers between devices with their start and end apart: 3, of which 3 were waited for; matrix products, arithmetic and copies ran while one was open for 0% of the time, Pallas kernels for 0%

profile of v1, /device:TPU:1, one launch (start us, length us, event | category | flops | bytes accessed | tf_op | source)
XLA Modules:
  0.0 248.9 jit_solution(7479879113162187527)
XLA Ops:
  6.5 0.0 reduce-scatter.3.cloned.1.call-start
  6.5 0.8 compare_and_fusion
  7.3 0.8 subtract_convert_fusion
  8.1 0.8 fusion.23
  8.9 5.0 %broadcast_multiply_fusion = f32[8192,128]{1,0:T(8,128)S(1)} fusion(f32[8192,128]{1,0:T(8,128)} %param.3, f32[8192]{0:T(1024)S(1)} %subtract_convert_fusion), kind=kLoop, calls=%fused_computation.5 | loop fusion | flops 1048576 | bytes 8421376 | tf_op jit(solution)/shard_map/mul | solution.py:18
  13.9 8.4 %fusion.7 = f32[64,128,128]{2,1,0:T(8,128)} fusion(f32[64,128,128]{2,1,0:T(8,128)S(1)} %bitcast.15), kind=kOutput, calls=%fused_computation.15 | convolution fusion | flops 1611186176 | bytes 8388608 | tf_op jit(solution)/shard_map/ij,qjc->qic/dot_general | solution.py:20
  22.2 5.4 %copy.5 = f32[64,128,128]{1,0,2:T(8,128)} copy(f32[64,128,128]{2,1,0:T(8,128)} %fusion.7) | data formatting | bytes 8388608 | tf_op jit(solution)/shard_map/ij,qjc->qic/dot_general | solution.py:20
  27.6 5.5 %fusion = f32[64,128,128]{2,0,1:T(8,128)S(1)} fusion(f32[64,128,128]{1,0,2:T(8,128)} %copy.5), kind=kOutput, calls=%fused_computation.1 | convolution fusion | flops 805437440 | bytes 8388608 | tf_op jit(solution)/shard_map/pq,qic->pic/dot_general | solution.py:21
  33.2 4.4 %copy.4 = f32[64,128,128]{2,1,0:T(8,128)} copy(f32[64,128,128]{2,0,1:T(8,128)S(1)} %fusion) | data formatting | bytes 8388608 | tf_op jit(solution)/shard_map/pq,qic->pic/dot_general | solution.py:21
  37.5 30.1 %gather_fusion = f32[8192,128]{1,0:T(8,128)} fusion(f32[8192,128]{1,0:T(8,128)} %bitcast.14, s32[8192]{0:T(1024)S(1)} %get-tuple-element.6), kind=kCustom, calls=%fused_computation | custom fusion | bytes 8421376 | tf_op jit(solution)/shard_map/jit(_take)/gather | solution.py:47
  67.6 9.7 %select_multiply_fusion = f32[8192,128]{1,0:T(8,128)} fusion(f32[8192,128]{1,0:T(8,128)} %gather_fusion, f32[8192]{0:T(1024)S(1)} %get-tuple-element.5, pred[8192]{0:T(1024)(128)(4,1)S(1)} %compare_and_fusion), kind=kLoop, calls=%fused_computation.3 | loop fusion | flops 2097152 | bytes 8429568 | tf_op jit(solution)/shard_map/mul | solution.py:47
  77.3 0.0 reduce-scatter.3.cloned.1.call-update
  77.3 0.0 all-gather.2.cloned.1.call-start
  77.4 38.3 %reduce-scatter.3.cloned.1.call-done = f32[1024,128]{1,0:T(8,128)} async-done(((f32[8192,128]{1,0:T(8,128)}), f32[1024,128]{1,0:T(8,128)}) %reduce-scatter.3.cloned.1.call-update) | async-done | bytes 524304 | tf_op jit(solution)/shard_map/reduce_scatter | solution.py:48
  115.7 0.0 all-gather.2.cloned.1.call-update
  115.8 0.2 reduce-scatter.5.cloned.1.call-start
  116.0 79.7 %all-gather.2.cloned.1.call-done = f32[1024,2048]{1,0:T(8,128)} async-done(((f32[1024,128]{1,0:T(8,128)}), f32[1024,2048]{1,0:T(8,128)}) %all-gather.2.cloned.1.call-update) | async-done | bytes 8388624 | tf_op jit(solution)/shard_map/all_gather | solution.py:49
  195.6 16.5 %convolution_multiply_fusion = f32[2048,128]{1,0:T(8,128)} fusion(f32[1024,2048]{1,0:T(8,128)} %all-gather.2.cloned.1.call-done, f32[1024,128]{1,0:T(8,128)} %reduce-scatter.3.cloned.1.call-done), kind=kOutput, calls=%fused_computation.4 | convolution fusion | flops 3221487616 | bytes 9961472 | tf_op jit(solution)/shard_map/dot_general | solution.py:28
  212.1 0.0 reduce-scatter.5.cloned.1.call-update
  212.1 30.3 %reduce-scatter.5.cloned.1.call-done = f32[256,128]{1,0:T(8,128)} async-done(((f32[2048,128]{1,0:T(8,128)}), f32[256,128]{1,0:T(8,128)}) %reduce-scatter.5.cloned.1.call-update) | async-done | bytes 131088 | tf_op jit(solution)/shard_map/reduce_scatter | solution.py:50
Async XLA Ops:
  6.5 109.2 %reduce-scatter.3.cloned.1.call-start = ((), (), s32[]{:S(2)}) async-start(), calls=%async_computation.2 | async-start | bytes 4718592 | tf_op jit(solution)/shard_map/reduce_scatter | solution.py:48
  77.3 118.3 %all-gather.2.cloned.1.call-start = ((), (), s32[]{:S(2)}) async-start(), calls=%async_computation.3 | async-start | bytes 8912896 | tf_op jit(solution)/shard_map/all_gather | solution.py:49
  115.8 126.6 %reduce-scatter.5.cloned.1.call-start = ((), (), s32[]{:S(2)}) async-start(), calls=%async_computation.4 | async-start | bytes 1179648 | tf_op jit(solution)/shard_map/reduce_scatter | solution.py:50
Sparse Core Ops, SparseCore 0:
  77.5 38.2 reduce-scatter.2
  117.8 77.7 all-gather.1
  212.3 30.0 reduce-scatter.4

commit v2 on v1

v2 whole, which is shorter than its diff:
```python
import functools

import jax
import jax.numpy as jnp
from jax import lax
from jax.experimental import pallas as pl
from jax.experimental.pallas import tpu as pltpu
from jax.sharding import PartitionSpec as P

HEIGHT = 8192
SLOTS = 1024
GROUPS = 4
STEP = SLOTS // GROUPS
HALF = STEP // 2
WIDE = 128
MESH = pl.DeviceIdType.MESH


def parity_of(bits):
    bits = bits ^ (bits >> 4)
    bits = bits ^ (bits >> 2)
    bits = bits ^ (bits >> 1)
    return bits & 1


def split(value):
    high = value.astype(jnp.bfloat16)
    low = (value - high.astype(jnp.float32)).astype(jnp.bfloat16)
    return high, low


def kernel(
    codes, signs, slab, out,
    raw, table, mine, theirs, from_core, from_x1, from_x2, ybuf, zbuf,
    gram, core_gram, pieces, relay, arrive1, arrive2,
    load_sem, d_send, d_recv, x1_send, x1_recv, x2_send, x2_recv,
    y_send, y_recv, yf_send, yf_recv, z_send, z_recv, zf_send, zf_recv,
    c1_send, c1_recv, c2_send, c2_recv, c3_send, c3_recv,
):
    row = lax.axis_index("rows")
    col = lax.axis_index("cols")
    x, k = row // 2, row % 2
    y, z = col // 4, col % 4
    partner = (row + 1 - 2 * k, col)
    x_next = (((x + 1) % 4) * 2 + k, col)
    x_prev = (((x + 3) % 4) * 2 + k, col)
    y_next = (row, ((y + 1) % 4) * 4 + z)
    y_prev = (row, ((y + 3) % 4) * 4 + z)
    z_next = (row, y * 4 + (z + 1) % 4)
    z_prev = (row, y * 4 + (z + 3) % 4)

    loads = []
    for part in range(8):
        rows = pl.ds(part * 1024, 1024)
        loads.append(pltpu.make_async_copy(slab.at[rows], raw.at[rows], load_sem.at[part]))
        loads[-1].start()

    barrier = pltpu.get_barrier_semaphore()
    for other in (partner, x_next, x_prev, y_next, y_prev, z_next, z_prev):
        pl.semaphore_signal(barrier, inc=1, device_id=other, device_id_type=MESH)

    left = lax.broadcasted_iota(jnp.int32, (256, 256), 0)
    right = lax.broadcasted_iota(jnp.int32, (256, 256), 1)
    hadamard = (1 - 2 * parity_of(left & right)).astype(jnp.float32)

    def inside(q, carry):
        lower = hadamard[:, :128] * signs[pl.ds(2 * q, 1), :]
        upper = hadamard[:, 128:] * signs[pl.ds(2 * q + 1, 1), :]
        matrix = jnp.concatenate([lower, upper], axis=1).astype(jnp.bfloat16)
        start = pl.multiple_of(q * 256, 256)
        high, low = split(raw[pl.ds(start, 256), :])
        both = jnp.dot(
            matrix, jnp.concatenate([high, low], axis=1), preferred_element_type=jnp.float32
        )
        table[pl.ds(start, 256), :] = both[:, :128] + both[:, 128:]
        return carry

    for part in range(8):
        loads[part].wait()
        lax.fori_loop(part * 4, part * 4 + 4, inside, 0)

    def across(t, carry):
        starts = [pl.multiple_of(q * 256 + t * 8, 8) for q in range(32)]
        values = [table[pl.ds(start, 8), :] for start in starts]
        span = 1
        while span < 32:
            for base in range(0, 32, 2 * span):
                for i in range(base, base + span):
                    first, second = values[i], values[i + span]
                    values[i], values[i + span] = first + second, first - second
            span *= 2
        for start, value in zip(starts, values):
            table[pl.ds(start, 8), :] = value
            table[pl.ds(start + HEIGHT, 8), :] = -value
        return carry

    lax.fori_loop(0, 32, across, 0)

    pl.semaphore_wait(barrier, 7)

    def gather(g, d, core, target):
        base = (((x + d) % 4) * 2 + core) * SLOTS + g * STEP

        def eight(i, carry):
            at = pl.multiple_of(i * 8, 8)
            for u in range(8):
                target[pl.ds(at + u, 1), :] = table[pl.ds(codes[base + at + u], 1), :]
            return carry

        lax.fori_loop(0, STEP // 8, eight, 0)

    def remote(source, target, send, recv, device):
        return pltpu.make_async_remote_copy(
            src_ref=source, dst_ref=target, send_sem=send, recv_sem=recv,
            device_id=device, device_id_type=MESH,
        )

    sent = []

    def go(copy):
        copy.start()
        sent.append(copy)

    first, last = pl.ds(0, HALF), pl.ds(HALF, HALF)
    upper, lower = pl.ds(0, 64), pl.ds(64, 64)

    def core_copy(g, d):
        return remote(theirs.at[g, d], from_core.at[g, d], d_send.at[g, d], d_recv.at[g, d], partner)

    def x1_copy(g, side):
        rows, device = ((first, x_prev), (last, x_next))[side]
        return remote(
            mine.at[g, 2, rows], from_x1.at[g, side], x1_send.at[g, side], x1_recv.at[g, side], device
        )

    def x2_copy(g, side):
        d, device = ((3, x_prev), (1, x_next))[side]
        return remote(
            mine.at[g, d], from_x2.at[g, side], x2_send.at[g, side], x2_recv.at[g, side], device
        )

    def y_copy(g, side):
        device = (y_prev, y_next)[side]
        return remote(ybuf.at[g, y], ybuf.at[g, y], y_send.at[g, side], y_recv.at[g, side], device)

    def y_arrival(g, side):
        block = ((y + 1) % 4, (y + 3) % 4)[side]
        return remote(
            ybuf.at[g, block], ybuf.at[g, block], y_send.at[g, side], y_recv.at[g, side],
            (y_prev, y_next)[side],
        )

    def y_forward(g, side):
        block = ((y + 1) % 4, (y + 3) % 4)[side]
        rows, device = ((last, y_prev), (first, y_next))[side]
        return remote(
            ybuf.at[g, block, rows], ybuf.at[g, block, rows],
            yf_send.at[g, side], yf_recv.at[g, side], device,
        )

    def z_copy(g, side):
        device = (z_prev, z_next)[side]
        return remote(zbuf.at[g, z], zbuf.at[g, z], z_send.at[g, side], z_recv.at[g, side], device)

    def z_arrival(g, side):
        block = ((z + 1) % 4, (z + 3) % 4)[side]
        return remote(
            zbuf.at[g, block], zbuf.at[g, block], z_send.at[g, side], z_recv.at[g, side],
            (z_prev, z_next)[side],
        )

    def z_forward(g, side):
        block = ((z + 1) % 4, (z + 3) % 4)[side]
        rows, device = ((lower, z_prev), (upper, z_next))[side]
        return remote(
            zbuf.at[g, block, rows], zbuf.at[g, block, rows],
            zf_send.at[g, side], zf_recv.at[g, side], device,
        )

    def y_forwarded(g, side):
        rows = (last, first)[side]
        block = (y + 2) % 4
        return remote(
            ybuf.at[g, block, rows], ybuf.at[g, block, rows],
            yf_send.at[g, side], yf_recv.at[g, side], (y_prev, y_next)[side],
        )

    def z_forwarded(g, side):
        rows = (lower, upper)[side]
        block = (z + 2) % 4
        return remote(
            zbuf.at[g, block, rows], zbuf.at[g, block, rows],
            zf_send.at[g, side], zf_recv.at[g, side], (z_prev, z_next)[side],
        )

    def gather_one(g, d):
        gather(g, d, 1 - k, theirs.at[g, d])
        go(core_copy(g, d))
        gather(g, d, k, mine.at[g, d])

    def step1(g):
        gather_one(g, 2)
        core_copy(g, 2).wait_recv()
        mine[g, 2] = mine[g, 2] + from_core[g, 2]
        go(x1_copy(g, 0))
        go(x1_copy(g, 1))
        for d in (3, 1, 0):
            gather_one(g, d)

    def step2(g):
        x1_copy(g, 0).wait_recv()
        core_copy(g, 3).wait_recv()
        mine[g, 3, first] = mine[g, 3, first] + from_core[g, 3, first] + from_x1[g, 0]
        mine[g, 3, last] = mine[g, 3, last] + from_core[g, 3, last]
        go(x2_copy(g, 0))
        x1_copy(g, 1).wait_recv()
        core_copy(g, 1).wait_recv()
        mine[g, 1, first] = mine[g, 1, first] + from_core[g, 1, first]
        mine[g, 1, last] = mine[g, 1, last] + from_core[g, 1, last] + from_x1[g, 1]
        go(x2_copy(g, 1))

    def step3(g):
        core_copy(g, 0).wait_recv()
        x2_copy(g, 0).wait_recv()
        x2_copy(g, 1).wait_recv()
        block = mine[g, 0] + from_core[g, 0] + from_x2[g, 0] + from_x2[g, 1]
        ybuf[g, y] = block
        zbuf[g, z] = block.T
        go(y_copy(g, 0))
        go(y_copy(g, 1))
        go(z_copy(g, 0))
        go(z_copy(g, 1))

    def step4(g):
        for side in range(2):
            y_arrival(g, side).wait_recv()
            go(y_forward(g, side))
            z_arrival(g, side).wait_recv()
            go(z_forward(g, side))

    def step5(g):
        for side in range(2):
            y_forwarded(g, side).wait_recv()
            z_forwarded(g, side).wait_recv()
        for m in range(2):
            lhs = [split(zbuf[g, 2 * m + i]) for i in range(2)]
            lhs_high = jnp.concatenate([lhs[0][0], lhs[1][0]], axis=0)
            lhs_low = jnp.concatenate([lhs[0][1], lhs[1][1]], axis=0)
            for n in range(2):
                rhs = [split(ybuf[g, 2 * n + i]) for i in range(2)]
                rhs_high = jnp.concatenate([rhs[0][0], rhs[1][0]], axis=1)
                rhs_low = jnp.concatenate([rhs[0][1], rhs[1][1]], axis=1)
                product = functools.partial(jnp.dot, preferred_element_type=jnp.float32)
                value = (
                    product(lhs_high, rhs_high)
                    + product(lhs_high, rhs_low)
                    + product(lhs_low, rhs_high)
                )
                for i in range(2):
                    part = value[:, i * 128:(i + 1) * 128]
                    if g:
                        part = part + gram[2 * n + i, pl.ds(m * 256, 256), :]
                    gram[2 * n + i, pl.ds(m * 256, 256), :] = part

    stages = (step1, step2, step3, step4, step5)
    for turn in range(GROUPS + len(stages) - 1):
        for late, stage in enumerate(stages):
            if 0 <= turn - late < GROUPS:
                stage(turn - late)

    own_rows = pl.ds(pl.multiple_of(k * 256, 256), 256)
    other_rows = pl.ds(pl.multiple_of((1 - k) * 256, 256), 256)

    def c1_copy(d):
        at = (y + d) % 4
        return remote(gram.at[at, other_rows], core_gram.at[at], c1_send.at[d], c1_recv.at[d], partner)

    for d in (2, 3, 1, 0):
        go(c1_copy(d))

    def combined(d):
        c1_copy(d).wait_recv()
        at = (y + d) % 4
        gram[at, own_rows] = gram[at, own_rows] + core_gram[at]

    rows0, rows1 = pl.ds(0, 128), pl.ds(128, 128)
    k_rows = [
        pl.ds(pl.multiple_of(k * 256, 256), 128),
        pl.ds(pl.multiple_of(k * 256 + 128, 128), 128),
    ]

    def relay_copy(side):
        return remote(
            gram.at[(y + 2) % 4, k_rows[side]], relay.at[side],
            c2_send.at[side], c2_recv.at[side], (y_prev, y_next)[side],
        )

    def relay_on(side):
        block = ((y + 1) % 4, (y + 3) % 4)[side]
        return remote(
            relay.at[side], pieces.at[block, (rows0, rows1)[side]],
            c2_send.at[2 + side], c2_recv.at[2 + side], (y_prev, y_next)[side],
        )

    def relayed(side):
        return remote(
            relay.at[side], pieces.at[(y + 2) % 4, (rows0, rows1)[side]],
            c2_send.at[2 + side], c2_recv.at[2 + side], (y_prev, y_next)[side],
        )

    def near_copy(side):
        at = ((y + 3) % 4, (y + 1) % 4)[side]
        return remote(
            gram.at[at, own_rows], pieces.at[y],
            c2_send.at[4 + side], c2_recv.at[4 + side], (y_prev, y_next)[side],
        )

    def near_arrival(side):
        return remote(
            gram.at[y, own_rows], pieces.at[((y + 1) % 4, (y + 3) % 4)[side]],
            c2_send.at[4 + side], c2_recv.at[4 + side], (y_prev, y_next)[side],
        )

    combined(2)
    go(relay_copy(0))
    go(relay_copy(1))
    combined(3)
    go(near_copy(0))
    combined(1)
    go(near_copy(1))
    for side in range(2):
        relay_copy(side).wait_recv()
        go(relay_on(side))
    c1_copy(0).wait_recv()
    pieces[y] = gram[y, own_rows] + core_gram[y]
    for side in range(2):
        near_arrival(side).wait_recv()
    for side in range(2):
        relayed(side).wait_recv()

    def c3_first(side):
        return remote(
            pieces.at[(x + 2) % 4, (rows0, rows1)[side]], arrive1.at[side],
            c3_send.at[side], c3_recv.at[side], (x_prev, x_next)[side],
        )

    def c3_second(side):
        return remote(
            pieces.at[((x + 3) % 4, (x + 1) % 4)[side]], arrive2.at[side],
            c3_send.at[2 + side], c3_recv.at[2 + side], (x_prev, x_next)[side],
        )

    for side in range(2):
        go(c3_first(side))
    for side in range(2):
        c3_first(side).wait_recv()
        at = ((x + 3) % 4, (x + 1) % 4)[side]
        rows = (rows0, rows1)[side]
        pieces[at, rows] = pieces[at, rows] + arrive1[side]
        go(c3_second(side))
    for side in range(2):
        c3_second(side).wait_recv()
    out[...] = (pieces[x] + arrive2[0] + arrive2[1]) * (1.0 / (8 * SLOTS * 8 * HEIGHT))

    for copy in sent:
        copy.wait_send()


def shards(slab, sign_bits, sample_rows):
    me = lax.axis_index("rows")
    parity = parity_of((sample_rows // HEIGHT) & me)
    codes = sample_rows % HEIGHT + HEIGHT * parity
    signs = (1 - 2 * sign_bits).astype(jnp.float32).reshape(64, 128)
    dma = pltpu.SemaphoreType.DMA
    f32 = functools.partial(pltpu.VMEM, dtype=jnp.float32)
    vmem = lambda *shape: pltpu.VMEM(shape, jnp.float32)
    return pl.pallas_call(
        kernel,
        out_shape=jax.ShapeDtypeStruct((256, 128), jnp.float32),
        in_specs=[
            pl.BlockSpec(memory_space=pltpu.SMEM),
            pl.BlockSpec(memory_space=pltpu.VMEM),
            pl.BlockSpec(memory_space=pl.ANY),
        ],
        out_specs=pl.BlockSpec(memory_space=pltpu.VMEM),
        scratch_shapes=[
            vmem(HEIGHT, WIDE),
            vmem(2 * HEIGHT, WIDE),
            vmem(GROUPS, 4, STEP, WIDE),
            vmem(GROUPS, 4, STEP, WIDE),
            vmem(GROUPS, 4, STEP, WIDE),
            vmem(GROUPS, 2, HALF, WIDE),
            vmem(GROUPS, 2, STEP, WIDE),
            vmem(GROUPS, 4, STEP, WIDE),
            vmem(GROUPS, 4, WIDE, STEP),
            vmem(4, 512, WIDE),
            vmem(4, 256, WIDE),
            vmem(4, 256, WIDE),
            vmem(2, 128, WIDE),
            vmem(2, 128, WIDE),
            vmem(2, 256, WIDE),
            dma((8,)),
            dma((GROUPS, 4)), dma((GROUPS, 4)),
            dma((GROUPS, 2)), dma((GROUPS, 2)),
            dma((GROUPS, 2)), dma((GROUPS, 2)),
            dma((GROUPS, 2)), dma((GROUPS, 2)),
            dma((GROUPS, 2)), dma((GROUPS, 2)),
            dma((GROUPS, 2)), dma((GROUPS, 2)),
            dma((GROUPS, 2)), dma((GROUPS, 2)),
            dma((4,)), dma((4,)),
            dma((6,)), dma((6,)),
            dma((4,)), dma((4,)),
        ],
        compiler_params=pltpu.CompilerParams(
            collective_id=0, has_side_effects=True, vmem_limit_bytes=56 * 1024 * 1024
        ),
        name="sketch",
    )(codes, signs, slab)


def solution(mesh):
    return jax.shard_map(
        shards,
        mesh=mesh,
        in_specs=(P("rows", "cols"), P("rows"), P()),
        out_specs=P("rows", "cols"),
        check_vma=False,
    )
```

time: 252 us -> 76.1 us (0.30); the launches traced: 249 us -> 75.7 us
  waiting for transfers between devices: 148 us -> 0 us
  Pallas kernels: 0 us -> 71.4 us
  local copies, waits for them, and re-layouts: 39.8 us -> 1.57 us
  matrix products: 30.3 us -> 0 us
  other arithmetic: 17 us -> 2.78 us
  between operations: 13.1 us -> 0.01 us
    all_gather x1 -> x0, waiting for transfers between devices: 79.7 us -> none  [shards(): lax.all_gather(picked, 'cols', axis=1, tiled=True)]
    pallas_call x0 -> x1, Pallas kernels: none -> 71.4 us  [shards(): pl.pallas_call(kernel, out_shape=jax.ShapeDtypeStruct((256, 128), jnp.flo...]
    reduce_scatter x2 -> x0, waiting for transfers between devices: 68.6 us -> none  [the longest x1 38.3 us: shards(): picked = lax.psum_scatter(terms, 'rows', scatter_dimension=0, tiled=True)]
    dot_general x3 -> x0, matrix products: 30.3 us -> none  [the longest x1 16.5 us: column_product(): lax.dot_general(portion, own_rows, (((0,), (0,)), ((), ())), precision=la...]
    gather x1 -> x0, local copies, waits for them, and re-layouts: 30.1 us -> none  [shards(): jnp.take(local, offsets, axis=0)]
    mul x2 -> x0, other arithmetic: 14.7 us -> none  [the longest x1 9.71 us: shards(): jnp.take(local, offsets, axis=0)]
    dot_general x2 -> x0, local copies, waits for them, and re-layouts: 9.77 us -> none  [the longest x1 5.4 us: local_transform(): jnp.einsum('ij,qjc->qic', parity_table(128), blocks, precision=lax.Precis...]
  transfers between devices with their start and end apart: 3 -> 0, of which waited for: 3 -> 0; matrix products, arithmetic and copies ran while one was open for 0% -> 0% of each run, Pallas kernels for 0% -> 0%
where the time goes in v2:
time: 76.1 us; the launch traced here: 75.7 us
  Pallas kernels  71.4 us (94%)
  other arithmetic  2.78 us (4%)
  local copies, waits for them, and re-layouts  1.57 us (2%)
    pallas_call x1, Pallas kernels, shards(): pl.pallas_call(kernel, out_shape=jax.ShapeDtypeStruct((256, 128), jnp.flo...  71.4 us
    unnamed x1, local copies, waits for them, and re-layouts  1.57 us

profile of v2, /device:TPU:1, one launch (start us, length us, event | category | flops | bytes accessed | tf_op | source)
XLA Modules:
  0.0 75.7 jit_solution(15597513858344456742)
XLA Ops:
  0.0 1.4 %fusion.codes = s32[8192]{0:T(1024)} fusion(s32[8192]{0:T(1024)} %param.5, s32[]{:T(128)S(6)} %axis_index.15), kind=kLoop, calls=%fused_computation.8 | loop fusion | flops 237568 | bytes 65540 | tf_op jit(solution)/shard_map/add | solution.py:372
  1.4 1.4 %convert_bitcast_fusion.signs = f32[64,128]{1,0:T(8,128)} fusion(s32[8192]{0:T(1024)} %param.4), kind=kLoop, calls=%fused_computation.12 | loop fusion | flops 24576 | bytes 65536 | tf_op jit(solution)/shard_map/reshape | solution.py:373
  2.8 71.4 %sketch.1 = f32[256,128]{1,0:T(8,128)} custom-call(s32[8192]{0:T(1024)} %fusion.codes, f32[64,128]{1,0:T(8,128)} %convert_bitcast_fusion.signs, f32[8192,128]{1,0:T(8,128)} %slab.1), custom_call_target="tpu_custom_call" | custom-call | tf_op jit(solution)/shard_map/sketch/pallas_call | solution.py:377
  74.2 1.6 %copy.5 = f32[256,128]{1,0:T(8,128)} copy(f32[256,128]{1,0:T(8,128)} %sketch.1) | data formatting | bytes 262144

commit v3 on v1

v3 whole, which is shorter than its diff:
```python
import functools

import jax
import jax.numpy as jnp
from jax import lax
from jax.experimental import pallas as pl
from jax.experimental.pallas import tpu as pltpu
from jax.sharding import PartitionSpec as P

HEIGHT = 8192
SLOTS = 1024
GROUPS = 8
STEP = SLOTS // GROUPS
HALF = STEP // 2
WIDE = 128
MESH = pl.DeviceIdType.MESH
SCALE = 1.0 / (8 * SLOTS * 8 * HEIGHT)

ORDER = (
    (0, 0, 2), (0, 1, 2), (0, 0, 0), (0, 2, 2), (0, 0, 3), (1, 0, 0), (0, 0, 1), (1, 1, 0),
    (0, 1, 0), (1, 2, 0), (0, 3, 2), (2, 0, 0), (0, 1, 3), (2, 0, 1), (0, 1, 1), (0, 2, 0),
    (0, 4, 2), (1, 3, 0), (0, 2, 3), (2, 1, 0), (0, 2, 1), (3, 0, 0), (3, 0, 1), (2, 1, 1),
    (0, 3, 0), (1, 4, 0), (0, 5, 2), (3, 1, 0), (3, 1, 1), (2, 2, 0), (0, 3, 3), (2, 2, 1),
    (0, 3, 1), (3, 2, 0), (3, 2, 1), (0, 4, 0), (1, 5, 0), (0, 6, 2), (2, 3, 0), (0, 4, 3),
    (2, 3, 1), (0, 4, 1), (3, 3, 0), (3, 3, 1), (0, 5, 0), (1, 6, 0), (0, 7, 2), (2, 4, 0),
    (0, 5, 3), (2, 4, 1), (4, 0, 0), (0, 5, 1), (0, 6, 0), (1, 7, 0), (3, 4, 0), (3, 4, 1),
    (0, 6, 3), (2, 5, 0), (0, 6, 1), (4, 1, 0), (2, 5, 1), (0, 7, 0), (0, 7, 3), (2, 6, 0),
    (0, 7, 1), (4, 2, 0), (2, 6, 1), (3, 5, 0), (3, 5, 1), (2, 7, 0), (2, 7, 1), (5, 0, 0),
    (5, 0, 1), (5, 0, 2), (5, 0, 3), (4, 3, 0), (5, 1, 0), (5, 1, 1), (5, 1, 2), (5, 1, 3),
    (3, 6, 0), (3, 6, 1), (5, 2, 0), (5, 2, 1), (5, 2, 2), (5, 2, 3), (3, 7, 0), (3, 7, 1),
    (6, 0, 0), (4, 4, 0), (5, 3, 0), (5, 3, 1), (5, 3, 2), (5, 3, 3), (6, 1, 0), (4, 5, 0),
    (6, 2, 0), (4, 6, 0), (4, 7, 0), (5, 4, 0), (5, 4, 1), (5, 4, 2), (5, 4, 3), (6, 3, 0),
    (5, 5, 0), (5, 5, 1), (5, 5, 2), (5, 5, 3), (5, 6, 0), (5, 6, 1), (5, 6, 2), (5, 6, 3),
    (5, 7, 0), (5, 7, 1), (5, 7, 2), (5, 7, 3), (6, 4, 0), (6, 5, 0), (6, 6, 0), (6, 7, 0),
)


def parity_of(bits):
    bits = bits ^ (bits >> 4)
    bits = bits ^ (bits >> 2)
    bits = bits ^ (bits >> 1)
    return bits & 1


def split(value):
    high = value.astype(jnp.bfloat16)
    low = (value - high.astype(jnp.float32)).astype(jnp.bfloat16)
    return high, low


def kernel(
    samples, bits, slab, out,
    raw, table, matrix, code_rows, codes, mine, theirs, from_core, from_x1, from_x2, ybuf, zbuf,
    gram, core_gram, from_c1, from_c2, final, arrived,
    load_sem, code_sem, d_send, d_recv, x1_send, x1_recv, x2_send, x2_recv,
    y_send, y_recv, yf_send, yf_recv, z_send, z_recv, zf_send, zf_recv,
    c1_send, c1_recv, c2_send, c2_recv, c3_send, c3_recv, c4_send, c4_recv,
):
    row = lax.axis_index("rows")
    col = lax.axis_index("cols")
    x, k = row // 2, row % 2
    y, z = col // 4, col % 4
    partner = (row + 1 - 2 * k, col)
    x_sides = ((((x + 3) % 4) * 2 + k, col), (((x + 1) % 4) * 2 + k, col))
    y_sides = ((row, ((y + 3) % 4) * 4 + z), (row, ((y + 1) % 4) * 4 + z))
    z_sides = ((row, y * 4 + (z + 3) % 4), (row, y * 4 + (z + 1) % 4))
    owners = [(x * 2 + z // 2, y * 4 + 2 * k + j) for j in range(2)]

    loads = []
    for part in range(8):
        rows = pl.ds(part * 1024, 1024)
        loads.append(pltpu.make_async_copy(slab.at[rows], raw.at[rows], load_sem.at[part]))
        loads[-1].start()

    barrier = pltpu.get_barrier_semaphore()
    for other in (partner, *x_sides, *y_sides, *z_sides):
        pl.semaphore_signal(barrier, inc=1, device_id=other, device_id_type=MESH)
    for j in range(2):
        @pl.when(2 * k + j != z)
        def _():
            pl.semaphore_signal(barrier, inc=1, device_id=owners[j], device_id_type=MESH)

    code_rows[...] = samples[...] % HEIGHT + HEIGHT * parity_of((samples[...] // HEIGHT) & row)

    left = lax.broadcasted_iota(jnp.int32, (256, 256), 0)
    right = lax.broadcasted_iota(jnp.int32, (256, 256), 1)
    matrix[...] = (1 - 2 * parity_of(left & right)).astype(jnp.float32).astype(jnp.bfloat16)

    def inside(q):
        signs = [
            (1 - 2 * bits[pl.ds(2 * q + i, 1), :]).astype(jnp.float32).astype(jnp.bfloat16)
            for i in range(2)
        ]
        signed = matrix[...] * jnp.concatenate(signs, axis=1)
        start = pl.multiple_of(q * 256, 256)
        high, low = split(raw[pl.ds(start, 256), :])
        both = jnp.dot(
            signed, jnp.concatenate([high, low], axis=1), preferred_element_type=jnp.float32
        )
        table[pl.ds(start, 256), :] = both[:, :128] + both[:, 128:]

    def two_inside(i, carry):
        inside(2 * i)
        inside(2 * i + 1)
        return carry

    code_copy = pltpu.make_async_copy(code_rows, codes, code_sem)
    for part in range(8):
        loads[part].wait()
        lax.fori_loop(part * 2, part * 2 + 2, two_inside, 0)
        if part == 1:
            code_copy.start()

    def across(t, carry):
        starts = [pl.multiple_of(q * 256 + t * 8, 8) for q in range(32)]
        values = [table[pl.ds(start, 8), :] for start in starts]
        span = 1
        while span < 32:
            for base in range(0, 32, 2 * span):
                for i in range(base, base + span):
                    first, second = values[i], values[i + span]
                    values[i], values[i + span] = first + second, first - second
            span *= 2
        for start, value in zip(starts, values):
            table[pl.ds(start, 8), :] = value
            table[pl.ds(start + HEIGHT, 8), :] = -value
        return carry

    lax.fori_loop(0, 32, across, 0)
    code_copy.wait()

    pl.semaphore_wait(barrier, 8 + (z // 2 - k) * (z // 2 - k))

    def gather(g, d, core, target):
        base = (((x + d) % 4) * 2 + core) * SLOTS + g * STEP

        def eight(i, carry):
            at = base + i * 8
            to = pl.multiple_of(g * STEP + i * 8, 8)
            for u in range(8):
                target[d, pl.ds(to + u, 1), :] = table[pl.ds(codes[at + u], 1), :]
            return carry

        lax.fori_loop(0, STEP // 8, eight, 0)

    def remote(source, target, send, recv, device):
        return pltpu.make_async_remote_copy(
            src_ref=source, dst_ref=target, send_sem=send, recv_sem=recv,
            device_id=device, device_id_type=MESH,
        )

    sent = []

    def go(copy):
        copy.start()
        sent.append(copy)

    def slots(g):
        return pl.ds(g * STEP, STEP)

    def half(g, side):
        return pl.ds(g * STEP + side * HALF, HALF)

    distances = (3, 1)

    def core_copy(g, d):
        return remote(
            theirs.at[d, slots(g)], from_core.at[d, slots(g)],
            d_send.at[g, d], d_recv.at[g, d], partner,
        )

    def x1_copy(g, side):
        return remote(
            mine.at[2, half(g, side)], from_x1.at[side, pl.ds(g * HALF, HALF)],
            x1_send.at[g, side], x1_recv.at[g, side], x_sides[side],
        )

    def x2_copy(g, side, late):
        rows = half(g, side if late else 1 - side)
        return remote(
            mine.at[distances[side], rows], from_x2.at[side, rows],
            x2_send.at[g, side, late], x2_recv.at[g, side, late], x_sides[side],
        )

    def z_near(g, side, block):
        return remote(
            zbuf.at[block, slots(g)], zbuf.at[block, slots(g)],
            z_send.at[g, side], z_recv.at[g, side], z_sides[side],
        )

    def z_far(g, side, block):
        return remote(
            zbuf.at[block, half(g, side)], zbuf.at[block, half(g, side)],
            zf_send.at[g, side], zf_recv.at[g, side], z_sides[side],
        )

    def y_near(g, side, block):
        return remote(
            ybuf.at[g, block], ybuf.at[g, block],
            y_send.at[g, side], y_recv.at[g, side], y_sides[side],
        )

    def y_far(g, side, block):
        rows = pl.ds(64 * side, 64)
        return remote(
            ybuf.at[g, block, rows], ybuf.at[g, block, rows],
            yf_send.at[g, side], yf_recv.at[g, side], y_sides[side],
        )

    def came(at, side):
        return ((at + 1) % 4, (at + 3) % 4)[side]

    def take_rows(g, d):
        gather(g, d, 1 - k, theirs)
        go(core_copy(g, d))
        gather(g, d, k, mine)

    def send_x1(g, _):
        core_copy(g, 2).wait_recv()
        mine[2, slots(g)] = mine[2, slots(g)] + from_core[2, slots(g)]
        go(x1_copy(g, 0))
        go(x1_copy(g, 1))

    def send_x2_early(g, side):
        d = distances[side]
        core_copy(g, d).wait_recv()
        mine[d, slots(g)] = mine[d, slots(g)] + from_core[d, slots(g)]
        go(x2_copy(g, side, 0))

    def send_x2_late(g, side):
        d = distances[side]
        x1_copy(g, side).wait_recv()
        rows = half(g, side)
        mine[d, rows] = mine[d, rows] + from_x1[side, pl.ds(g * HALF, HALF)]
        go(x2_copy(g, side, 1))

    def send_yz(g, _):
        core_copy(g, 0).wait_recv()
        for side in range(2):
            for late in range(2):
                x2_copy(g, side, late).wait_recv()
        rows = slots(g)
        block = (mine[0, rows] + from_core[0, rows]) + (from_x2[0, rows] + from_x2[1, rows])
        zbuf[z, rows] = block
        ybuf[g, y] = block.T
        for side in range(2):
            go(z_near(g, side, z))
            go(y_near(g, side, y))

    def forward(g, which):
        side = which % 2
        if which < 2:
            y_near(g, side, came(y, side)).wait_recv()
            go(y_far(g, side, came(y, side)))
        else:
            z_near(g, side, came(z, side)).wait_recv()
            go(z_far(g, side, came(z, side)))

    def multiply(g, _):
        for side in range(2):
            y_far(g, side, (y + 2) % 4).wait_recv()
            z_far(g, side, (z + 2) % 4).wait_recv()
        right = []
        for h in range(2):
            high, low = split(
                jnp.concatenate([zbuf[2 * h, slots(g)], zbuf[2 * h + 1, slots(g)]], axis=1)
            )
            right.append(jnp.concatenate([high, low, high], axis=0))
        for m in range(2):
            high, low = split(
                jnp.concatenate([ybuf[g, 2 * m], ybuf[g, 2 * m + 1]], axis=0)
            )
            left = jnp.concatenate([high, high, low], axis=1)
            for h in range(2):
                value = jnp.dot(left, right[h], preferred_element_type=jnp.float32)
                for i in range(2):
                    part = value[i * 128:(i + 1) * 128]
                    if g:
                        part = part + gram[2 * m + i, h]
                    gram[2 * m + i, h] = part

    steps = (take_rows, send_x1, send_x2_early, send_x2_late, send_yz, forward, multiply)
    for kind, group, side in ORDER:
        steps[kind](group, side)

    def c1_copy(d):
        at = (x + d) % 4
        return remote(
            gram.at[at, 1 - k], core_gram.at[at], c1_send.at[d], c1_recv.at[d], partner
        )

    def combine(d):
        at = (x + d) % 4
        c1_copy(d).wait_recv()
        core_gram[at] = core_gram[at] + gram[at, k]

    def c2_copy(side):
        return remote(
            core_gram.at[(x + 2) % 4, pl.ds(64 * side, 64)], from_c1.at[side],
            c2_send.at[side], c2_recv.at[side], x_sides[side],
        )

    def c3_copy(side, late):
        rows = pl.ds(64 * (side if late else 1 - side), 64)
        return remote(
            core_gram.at[(x + distances[side]) % 4, rows], from_c2.at[side, rows],
            c3_send.at[side, late], c3_recv.at[side, late], x_sides[side],
        )

    for d in (2, 3, 1, 0):
        go(c1_copy(d))
    combine(2)
    for side in range(2):
        go(c2_copy(side))
    for side in range(2):
        combine(distances[side])
        go(c3_copy(side, 0))
    combine(0)
    for side in range(2):
        c2_copy(side).wait_recv()
        at = (x + distances[side]) % 4
        rows = pl.ds(64 * side, 64)
        core_gram[at, rows] = core_gram[at, rows] + from_c1[side]
        go(c3_copy(side, 1))
    for side in range(2):
        for late in range(2):
            c3_copy(side, late).wait_recv()
    total = (core_gram[x] + (from_c2[0] + from_c2[1])) * SCALE

    def c4_copy(j, slot):
        return remote(
            final.at[j], arrived.at[slot], c4_send.at[j], c4_recv.at[slot], owners[j]
        )

    for j in range(2):
        final[j] = total[:, j * 128:(j + 1) * 128]
    for j in range(2):
        @pl.when(2 * k + j != z)
        def _():
            c4_copy(j, z % 2).start()

        @pl.when(2 * k + j == z)
        def _():
            out[pl.ds(j * 128, 128), :] = total[:, j * 128:(j + 1) * 128]

    for copy in sent:
        copy.wait_send()
    for j in range(2):
        @pl.when(2 * k + j != z)
        def _():
            c4_copy(j, j).wait_recv()
            out[pl.ds(j * 128, 128), :] = arrived[j]
            c4_copy(j, j).wait_send()


def shards(slab, sign_bits, sample_rows):
    dma = pltpu.SemaphoreType.DMA
    vmem = lambda *shape: pltpu.VMEM(shape, jnp.float32)
    pairs = [dma((GROUPS, 2))] * 2
    return pl.pallas_call(
        kernel,
        out_shape=jax.ShapeDtypeStruct((256, 128), jnp.float32),
        in_specs=[
            pl.BlockSpec(memory_space=pltpu.VMEM),
            pl.BlockSpec(memory_space=pltpu.VMEM),
            pl.BlockSpec(memory_space=pl.ANY),
        ],
        out_specs=pl.BlockSpec(memory_space=pltpu.VMEM),
        scratch_shapes=[
            vmem(HEIGHT, WIDE),
            vmem(2 * HEIGHT, WIDE),
            pltpu.VMEM((256, 256), jnp.bfloat16),
            pltpu.VMEM((8 * SLOTS,), jnp.int32),
            pltpu.SMEM((8 * SLOTS,), jnp.int32),
            vmem(4, SLOTS, WIDE),
            vmem(4, SLOTS, WIDE),
            vmem(4, SLOTS, WIDE),
            vmem(2, SLOTS // 2, WIDE),
            vmem(2, SLOTS, WIDE),
            vmem(GROUPS, 4, WIDE, STEP),
            vmem(4, SLOTS, WIDE),
            vmem(4, 2, 128, 256),
            vmem(4, 128, 256),
            vmem(2, 64, 256),
            vmem(2, 128, 256),
            vmem(2, 128, 128),
            vmem(2, 128, 128),
            dma((8,)), dma(()),
            dma((GROUPS, 4)), dma((GROUPS, 4)),
            *pairs,
            dma((GROUPS, 2, 2)), dma((GROUPS, 2, 2)),
            *pairs, *pairs, *pairs, *pairs,
            dma((4,)), dma((4,)),
            dma((2,)), dma((2,)),
            dma((2, 2)), dma((2, 2)),
            dma((2,)), dma((2,)),
        ],
        compiler_params=pltpu.CompilerParams(
            collective_id=0, has_side_effects=True, vmem_limit_bytes=56 * 1024 * 1024
        ),
        name="sketch",
    )(sample_rows, sign_bits.reshape(64, 128), slab)


def solution(mesh):
    return jax.shard_map(
        shards,
        mesh=mesh,
        in_specs=(P("rows", "cols"), P("rows"), P()),
        out_specs=P("rows", "cols"),
        check_vma=False,
    )
```

time: 252 us -> 62.6 us (0.25); the launches traced: 249 us -> 62.4 us
  waiting for transfers between devices: 148 us -> 0 us
  Pallas kernels: 0 us -> 60.8 us
  local copies, waits for them, and re-layouts: 39.8 us -> 1.57 us
  matrix products: 30.3 us -> 0 us
  other arithmetic: 17 us -> 0 us
  between operations: 13.1 us -> 0.01 us
    all_gather x1 -> x0, waiting for transfers between devices: 79.7 us -> none  [shards(): lax.all_gather(picked, 'cols', axis=1, tiled=True)]
    reduce_scatter x2 -> x0, waiting for transfers between devices: 68.6 us -> none  [the longest x1 38.3 us: shards(): picked = lax.psum_scatter(terms, 'rows', scatter_dimension=0, tiled=True)]
    pallas_call x0 -> x1, Pallas kernels: none -> 60.8 us  [shards(): pl.pallas_call(kernel, out_shape=jax.ShapeDtypeStruct((256, 128), jnp.flo...]
    dot_general x3 -> x0, matrix products: 30.3 us -> none  [the longest x1 16.5 us: column_product(): lax.dot_general(portion, own_rows, (((0,), (0,)), ((), ())), precision=la...]
    gather x1 -> x0, local copies, waits for them, and re-layouts: 30.1 us -> none  [shards(): jnp.take(local, offsets, axis=0)]
    mul x2 -> x0, other arithmetic: 14.7 us -> none  [the longest x1 9.71 us: shards(): jnp.take(local, offsets, axis=0)]
    dot_general x2 -> x0, local copies, waits for them, and re-layouts: 9.77 us -> none  [the longest x1 5.4 us: local_transform(): jnp.einsum('ij,qjc->qic', parity_table(128), blocks, precision=lax.Precis...]
  transfers between devices with their start and end apart: 3 -> 0, of which waited for: 3 -> 0; matrix products, arithmetic and copies ran while one was open for 0% -> 0% of each run, Pallas kernels for 0% -> 0%
where the time goes in v3:
time: 62.6 us; the launch traced here: 62.4 us
  Pallas kernels  60.8 us (97%)
  local copies, waits for them, and re-layouts  1.57 us (3%)
    pallas_call x1, Pallas kernels, shards(): pl.pallas_call(kernel, out_shape=jax.ShapeDtypeStruct((256, 128), jnp.flo...  60.8 us
    unnamed x1, local copies, waits for them, and re-layouts  1.57 us

profile of v3, /device:TPU:1, one launch (start us, length us, event | category | flops | bytes accessed | tf_op | source)
XLA Modules:
  0.0 62.4 jit_solution(8585978615939432631)
XLA Ops:
  0.0 60.8 %sketch.1 = f32[256,128]{1,0:T(8,128)} custom-call(s32[8192]{0:T(1024)} %samples.1, s32[64,128]{1,0:T(8,128)} %bitcast.1, f32[8192,128]{1,0:T(8,128)} %slab.1), custom_call_target="tpu_custom_call" | custom-call | tf_op jit(solution)/shard_map/sketch/pallas_call | solution.py:360
  60.8 1.6 %copy.5 = f32[256,128]{1,0:T(8,128)} copy(f32[256,128]{1,0:T(8,128)} %sketch.1) | data formatting | bytes 262144

commit v4 on v3

v4 whole, which is shorter than its diff:
```python
import functools

import jax
import jax.numpy as jnp
from jax import lax
from jax.experimental import pallas as pl
from jax.experimental.pallas import tpu as pltpu
from jax.sharding import PartitionSpec as P

HEIGHT = 8192
SLOTS = 1024
GROUPS = 8
STEP = SLOTS // GROUPS
HALF = STEP // 2
PITCH = 264
NEGATED = HEIGHT // 256 * PITCH
WIDE = 128
MESH = pl.DeviceIdType.MESH
SCALE = 1.0 / (8 * SLOTS * 8 * HEIGHT)

ORDER = (
    (0, 0, 2), (0, 1, 2), (0, 0, 0), (0, 2, 2), (0, 1, 0), (0, 3, 2), (1, 0, 0), (0, 0, 1),
    (1, 1, 0), (0, 0, 3), (1, 2, 0), (0, 2, 0), (0, 4, 2), (1, 3, 0), (0, 1, 1), (2, 0, 1),
    (0, 1, 3), (2, 0, 0), (0, 3, 0), (0, 5, 2), (1, 4, 0), (0, 2, 1), (2, 1, 1), (0, 2, 3),
    (2, 1, 0), (0, 4, 0), (3, 0, 0), (0, 6, 2), (1, 5, 0), (0, 3, 1), (3, 1, 0), (2, 2, 1),
    (0, 3, 3), (2, 2, 0), (0, 5, 0), (3, 2, 0), (0, 7, 2), (1, 6, 0), (0, 4, 1), (2, 3, 1),
    (0, 4, 3), (2, 3, 0), (3, 3, 0), (0, 6, 0), (0, 5, 1), (1, 7, 0), (0, 5, 3), (2, 4, 1),
    (0, 7, 0), (2, 4, 0), (3, 4, 0), (0, 6, 1), (0, 6, 3), (2, 5, 1), (0, 7, 1), (2, 5, 0),
    (0, 7, 3), (4, 0, 0), (2, 6, 1), (2, 6, 0), (3, 5, 0), (2, 7, 1), (2, 7, 0), (4, 1, 0),
    (4, 2, 0), (3, 6, 0), (5, 0, 0), (5, 0, 1), (4, 3, 0), (5, 1, 0), (5, 1, 1), (3, 7, 0),
    (5, 2, 0), (5, 2, 1), (4, 4, 0), (5, 3, 0), (5, 3, 1), (4, 5, 0), (6, 1, 1), (4, 6, 0),
    (4, 7, 0), (5, 4, 0), (5, 4, 1), (6, 3, 1), (5, 5, 0), (5, 5, 1), (5, 6, 0), (5, 6, 1),
    (5, 7, 0), (5, 7, 1), (6, 5, 1), (6, 6, 0), (6, 7, 0),
)


def parity_of(bits):
    bits = bits ^ (bits >> 4)
    bits = bits ^ (bits >> 2)
    bits = bits ^ (bits >> 1)
    return bits & 1


def split(value):
    high = value.astype(jnp.bfloat16)
    low = (value - high.astype(jnp.float32)).astype(jnp.bfloat16)
    return high, low


def kernel(
    samples_in, bits_in, slab, out,
    samples, bits, raw, table, matrix, code_rows, codes, mine, theirs, from_core, from_x1, from_x2,
    ybuf, zbuf, gram, core_gram, from_c1, from_c2, final,
    load_sem, code_sem, d_recv, x1_recv, x2_recv, y_recv, z_recv, far_recv,
    c1_recv, c2_recv, c3_recv, c4_recv, c4_send,
    d_send, x1_send, x2_send, near_send, far_send, c1_send, c2_send, c3_send,
):
    row = lax.axis_index("rows")
    col = lax.axis_index("cols")
    x, k = row // 2, row % 2
    y, z = col // 4, col % 4
    partner = (row + 1 - 2 * k, col)
    x_sides = ((((x + 3) % 4) * 2 + k, col), (((x + 1) % 4) * 2 + k, col))
    y_sides = ((row, ((y + 3) % 4) * 4 + z), (row, ((y + 1) % 4) * 4 + z))
    z_sides = ((row, y * 4 + (z + 3) % 4), (row, y * 4 + (z + 1) % 4))
    owners = [(x * 2 + z // 2, y * 4 + 2 * k + j) for j in range(2)]

    loads = [
        pltpu.make_async_copy(bits_in, bits, load_sem.at[8]),
        pltpu.make_async_copy(samples_in, samples, load_sem.at[9]),
    ]
    for part in range(8):
        rows = pl.ds(part * 1024, 1024)
        loads.append(pltpu.make_async_copy(slab.at[rows], raw.at[rows], load_sem.at[part]))
    for load in (loads[0], loads[2], loads[1], *loads[3:]):
        load.start()

    barrier = pltpu.get_barrier_semaphore()
    for other in (partner, *x_sides, *y_sides, *z_sides):
        pl.semaphore_signal(barrier, inc=1, device_id=other, device_id_type=MESH)
    for j in range(2):
        @pl.when(2 * k + j != z)
        def _():
            pl.semaphore_signal(barrier, inc=1, device_id=owners[j], device_id_type=MESH)

    left = lax.broadcasted_iota(jnp.int32, (256, 256), 0)
    right = lax.broadcasted_iota(jnp.int32, (256, 256), 1)
    matrix[...] = (1 - 2 * parity_of(left & right)).astype(jnp.float32).astype(jnp.bfloat16)

    def inside(q):
        signs = [
            (1 - 2 * bits[pl.ds(2 * q + i, 1), :]).astype(jnp.float32).astype(jnp.bfloat16)
            for i in range(2)
        ]
        signed = matrix[...] * jnp.concatenate(signs, axis=1)
        start = pl.multiple_of(q * 256, 256)
        high, low = split(raw[pl.ds(start, 256), :])
        both = jnp.dot(
            signed, jnp.concatenate([high, low], axis=1), preferred_element_type=jnp.float32
        )
        table[pl.ds(pl.multiple_of(q * PITCH, 8), 256), :] = both[:, :128] + both[:, 128:]

    def four_inside(i, carry):
        for u in range(4):
            inside(4 * i + u)
        return carry

    code_copy = pltpu.make_async_copy(code_rows, codes, code_sem)
    loads[0].wait()
    for part in range(8):
        loads[2 + part].wait()
        four_inside(part, 0)
        if part == 1:
            loads[1].wait()
            parity = parity_of((samples[...] // HEIGHT) & row)
            offset = samples[...] % HEIGHT
            code_rows[...] = offset + offset // 256 * (PITCH - 256) + NEGATED * parity
        if part == 3:
            code_copy.start()

    def across(t, carry):
        starts = [pl.multiple_of(q * PITCH + t * 8, 8) for q in range(32)]
        values = [table[pl.ds(start, 8), :] for start in starts]
        span = 1
        while span < 32:
            for base in range(0, 32, 2 * span):
                for i in range(base, base + span):
                    first, second = values[i], values[i + span]
                    values[i], values[i + span] = first + second, first - second
            span *= 2
        for start, value in zip(starts, values):
            table[pl.ds(start, 8), :] = value
            table[pl.ds(start + NEGATED, 8), :] = -value
        return carry

    lax.fori_loop(0, 32, across, 0)
    code_copy.wait()

    pl.semaphore_wait(barrier, 8 + (z // 2 - k) * (z // 2 - k))

    def gather(g, d, core, target):
        base = (((x + d) % 4) * 2 + core) * SLOTS + g * STEP

        def some(i, carry):
            at = base + i * 32
            to = pl.multiple_of(g * STEP + i * 32, 32)
            for u in range(32):
                target[d, pl.ds(to + u, 1), :] = table[pl.ds(codes[at + u], 1), :]
            return carry

        lax.fori_loop(0, STEP // 32, some, 0)

    def remote(source, target, send, recv, device):
        return pltpu.make_async_remote_copy(
            src_ref=source, dst_ref=target, send_sem=send, recv_sem=recv,
            device_id=device, device_id_type=MESH,
        )

    def slots(g):
        return pl.ds(g * STEP, STEP)

    def half(g, side):
        return pl.ds(g * STEP + side * HALF, HALF)

    distances = (3, 1)

    def core_copy(g, d):
        return remote(
            theirs.at[d, slots(g)], from_core.at[d, slots(g)], d_send, d_recv.at[g, d], partner
        )

    def x1_copy(g, side):
        rows = half(g, side)
        return remote(mine.at[2, rows], from_x1.at[rows], x1_send, x1_recv.at[g], x_sides[side])

    def x2_copy(g, side, late):
        part = side if late else 1 - side
        return remote(
            mine.at[distances[side], half(g, part)], from_x2.at[g, side, pl.ds(part * HALF, HALF)],
            x2_send, x2_recv.at[g], x_sides[side],
        )

    def z_near(g, side):
        own = zbuf.at[z, slots(g)]
        return remote(own, own, near_send, z_recv.at[g], z_sides[side])

    def y_near(g, side):
        own = ybuf.at[g, y]
        return remote(own, own, near_send, y_recv.at[g], y_sides[side])

    def came(at, side):
        return ((at + 1) % 4, (at + 3) % 4)[side]

    def z_far(g, side):
        part = zbuf.at[came(z, side), half(g, side)]
        return remote(part, part, far_send, far_recv.at[g], z_sides[side])

    def y_far(g, side):
        part = ybuf.at[g, came(y, side), pl.ds(64 * side, 64)]
        return remote(part, part, far_send, far_recv.at[g], y_sides[side])

    def arrived(like, semaphore):
        remote(like, like, semaphore, semaphore, partner).wait_recv()

    def left_here(like, semaphore):
        remote(like, like, semaphore, semaphore, partner).wait_send()

    def take_rows(g, d):
        gather(g, d, 1 - k, theirs)
        core_copy(g, d).start()
        gather(g, d, k, mine)

    def send_x1(g, _):
        core_copy(g, 2).wait_recv()
        mine[2, slots(g)] = mine[2, slots(g)] + from_core[2, slots(g)]
        x1_copy(g, 0).start()
        x1_copy(g, 1).start()

    def send_x2_early(g, side):
        d = distances[side]
        core_copy(g, d).wait_recv()
        mine[d, slots(g)] = mine[d, slots(g)] + from_core[d, slots(g)]
        x2_copy(g, side, 0).start()

    def send_x2_late(g, _):
        arrived(from_x1.at[slots(g)], x1_recv.at[g])
        for side in range(2):
            d, rows = distances[side], half(g, side)
            mine[d, rows] = mine[d, rows] + from_x1[rows]
            x2_copy(g, side, 1).start()

    def send_yz(g, _):
        core_copy(g, 0).wait_recv()
        arrived(from_x2.at[g], x2_recv.at[g])
        rows = slots(g)
        block = (mine[0, rows] + from_core[0, rows]) + (from_x2[g, 0] + from_x2[g, 1])
        zbuf[z, rows] = block
        ybuf[g, y] = block.T
        for side in range(2):
            z_near(g, side).start()
            y_near(g, side).start()

    def forward(g, which):
        arrived(from_x2.at[g], (y_recv, z_recv)[which].at[g])
        for side in range(2):
            (y_far, z_far)[which](g, side).start()

    def multiply(g, more):
        groups = (g,) if not more else (g - 1, g)
        for each in groups:
            arrived(from_x2.at[each], far_recv.at[each])
        rows = pl.ds(groups[0] * STEP, STEP * len(groups))
        right = []
        for h in range(2):
            high, low = split(
                jnp.concatenate([zbuf[2 * h, rows], zbuf[2 * h + 1, rows]], axis=1)
            )
            right.append(jnp.concatenate([high, low, high], axis=0))
        for m in range(2):
            high, low = split(
                jnp.concatenate(
                    [
                        jnp.concatenate([ybuf[each, 2 * m], ybuf[each, 2 * m + 1]], axis=0)
                        for each in groups
                    ],
                    axis=1,
                )
            )
            left = jnp.concatenate([high, high, low], axis=1)
            for h in range(2):
                value = jnp.dot(left, right[h], preferred_element_type=jnp.float32)
                for i in range(2):
                    part = value[i * 128:(i + 1) * 128]
                    if groups[0]:
                        part = part + gram[2 * m + i, h]
                    gram[2 * m + i, h] = part

    steps = (take_rows, send_x1, send_x2_early, send_x2_late, send_yz, forward, multiply)
    for kind, group, side in ORDER:
        steps[kind](group, side)

    def c1_copy(d):
        at = (x + d) % 4
        return remote(gram.at[at, 1 - k], core_gram.at[at], c1_send, c1_recv.at[d], partner)

    def combine(d):
        at = (x + d) % 4
        c1_copy(d).wait_recv()
        core_gram[at] = core_gram[at] + gram[at, k]

    def c2_copy(side):
        rows = pl.ds(64 * side, 64)
        return remote(
            core_gram.at[(x + 2) % 4, rows], from_c1.at[rows], c2_send, c2_recv, x_sides[side]
        )

    def c3_copy(side, late):
        rows = pl.ds(64 * (side if late else 1 - side), 64)
        return remote(
            core_gram.at[(x + distances[side]) % 4, rows], from_c2.at[side, rows],
            c3_send, c3_recv, x_sides[side],
        )

    for d in (2, 3, 1, 0):
        c1_copy(d).start()
    combine(2)
    for side in range(2):
        c2_copy(side).start()
    for side in range(2):
        combine(distances[side])
        c3_copy(side, 0).start()
    combine(0)
    arrived(from_c1, c2_recv)
    for side in range(2):
        at = (x + distances[side]) % 4
        rows = pl.ds(64 * side, 64)
        core_gram[at, rows] = core_gram[at, rows] + from_c1[rows]
        c3_copy(side, 1).start()
    left_here(theirs, d_send)
    left_here(mine.at[2], x1_send)
    left_here(from_x2, x2_send)
    left_here(theirs, near_send)
    left_here(from_x2, far_send)
    arrived(from_c2, c3_recv)
    total = (core_gram[x] + (from_c2[0] + from_c2[1])) * SCALE

    def c4_copy(j, slot):
        return remote(
            final.at[j], out.at[pl.ds(pl.multiple_of(slot * 128, 128), 128)],
            c4_send.at[j], c4_recv.at[slot], owners[j],
        )

    def own_copy(j):
        return pltpu.make_async_copy(final.at[j], out.at[pl.ds(j * 128, 128)], c4_send.at[j])

    for j in range(2):
        final[j] = total[:, j * 128:(j + 1) * 128]
    for j in range(2):
        @pl.when(2 * k + j != z)
        def _():
            c4_copy(j, z % 2).start()

        @pl.when(2 * k + j == z)
        def _():
            own_copy(j).start()

    left_here(core_gram, c1_send)
    left_here(from_c1, c2_send)
    left_here(from_c2, c3_send)
    for j in range(2):
        @pl.when(2 * k + j != z)
        def _():
            c4_copy(j, j).wait()

        @pl.when(2 * k + j == z)
        def _():
            own_copy(j).wait()


def shards(slab, sign_bits, sample_rows):
    dma = pltpu.SemaphoreType.DMA
    vmem = lambda *shape: pltpu.VMEM(shape, jnp.float32)
    return pl.pallas_call(
        kernel,
        out_shape=jax.ShapeDtypeStruct((256, 128), jnp.float32),
        in_specs=[
            pl.BlockSpec(memory_space=pltpu.HBM),
            pl.BlockSpec(memory_space=pltpu.HBM),
            pl.BlockSpec(memory_space=pltpu.HBM),
        ],
        out_specs=pl.BlockSpec(memory_space=pltpu.HBM),
        scratch_shapes=[
            pltpu.VMEM((8 * SLOTS,), jnp.int32),
            pltpu.VMEM((HEIGHT // WIDE, WIDE), jnp.int32),
            vmem(HEIGHT, WIDE),
            vmem(2 * NEGATED, WIDE),
            pltpu.VMEM((256, 256), jnp.bfloat16),
            pltpu.VMEM((8 * SLOTS,), jnp.int32),
            pltpu.SMEM((8 * SLOTS,), jnp.int32),
            vmem(4, SLOTS, WIDE),
            vmem(4, SLOTS, WIDE),
            vmem(4, SLOTS, WIDE),
            vmem(SLOTS, WIDE),
            vmem(GROUPS, 2, STEP, WIDE),
            vmem(GROUPS, 4, WIDE, STEP),
            vmem(4, SLOTS, WIDE),
            vmem(4, 2, 128, 256),
            vmem(4, 128, 256),
            vmem(128, 256),
            vmem(2, 128, 256),
            vmem(2, 128, 128),
            dma((10,)), dma(()), dma((GROUPS, 4)),
            *[dma((GROUPS,))] * 5,
            dma((4,)), dma(()), dma(()), dma((2,)), dma((2,)),
            *[dma(())] * 8,
        ],
        compiler_params=pltpu.CompilerParams(
            collective_id=0, has_side_effects=True, vmem_limit_bytes=56 * 1024 * 1024
        ),
        name="sketch",
    )(sample_rows, sign_bits.reshape(64, 128), slab)


def solution(mesh):
    return jax.shard_map(
        shards,
        mesh=mesh,
        in_specs=(P("rows", "cols"), P("rows"), P()),
        out_specs=P("rows", "cols"),
        check_vma=False,
    )
```

time: 62.6 us -> 57.2 us (0.914)
  Pallas kernels: 60.8 us -> 55.6 us
    pallas_call x1, Pallas kernels: 60.8 us -> 55.6 us  [shards(): pl.pallas_call(kernel, out_shape=jax.ShapeDtypeStruct((256, 128), jnp.flo...]
where the time goes in v4:
time: 57.2 us; the launch traced here: 57.1 us
  Pallas kernels  55.6 us (97%)
  local copies, waits for them, and re-layouts  1.57 us (3%)
    pallas_call x1, Pallas kernels, shards(): pl.pallas_call(kernel, out_shape=jax.ShapeDtypeStruct((256, 128), jnp.flo...  55.6 us
    unnamed x1, local copies, waits for them, and re-layouts  1.57 us

profile of v4, /device:TPU:1, one launch (start us, length us, event | category | flops | bytes accessed | tf_op | source)
XLA Modules:
  0.0 57.1 jit_solution(18006672042352199689)
XLA Ops:
  0.0 55.6 %sketch.1 = f32[256,128]{1,0:T(8,128)} custom-call(s32[8192]{0:T(1024)} %samples_in.1, s32[64,128]{1,0:T(8,128)} %bitcast.1, f32[8192,128]{1,0:T(8,128)} %slab.1), custom_call_target="tpu_custom_call" | custom-call | tf_op jit(solution)/shard_map/sketch/pallas_call | solution.py:363
  55.6 1.6 %copy.5 = f32[256,128]{1,0:T(8,128)} copy(f32[256,128]{1,0:T(8,128)} %sketch.1) | data formatting | bytes 262144

commit v5 on v4

--- a/solution.py
+++ b/solution.py
@@ -19,18 +19,18 @@
 SCALE = 1.0 / (8 * SLOTS * 8 * HEIGHT)
 
 ORDER = (
-    (0, 0, 2), (0, 1, 2), (0, 0, 0), (0, 2, 2), (0, 1, 0), (0, 3, 2), (1, 0, 0), (0, 0, 1),
-    (1, 1, 0), (0, 0, 3), (1, 2, 0), (0, 2, 0), (0, 4, 2), (1, 3, 0), (0, 1, 1), (2, 0, 1),
-    (0, 1, 3), (2, 0, 0), (0, 3, 0), (0, 5, 2), (1, 4, 0), (0, 2, 1), (2, 1, 1), (0, 2, 3),
-    (2, 1, 0), (0, 4, 0), (3, 0, 0), (0, 6, 2), (1, 5, 0), (0, 3, 1), (3, 1, 0), (2, 2, 1),
-    (0, 3, 3), (2, 2, 0), (0, 5, 0), (3, 2, 0), (0, 7, 2), (1, 6, 0), (0, 4, 1), (2, 3, 1),
-    (0, 4, 3), (2, 3, 0), (3, 3, 0), (0, 6, 0), (0, 5, 1), (1, 7, 0), (0, 5, 3), (2, 4, 1),
-    (0, 7, 0), (2, 4, 0), (3, 4, 0), (0, 6, 1), (0, 6, 3), (2, 5, 1), (0, 7, 1), (2, 5, 0),
-    (0, 7, 3), (4, 0, 0), (2, 6, 1), (2, 6, 0), (3, 5, 0), (2, 7, 1), (2, 7, 0), (4, 1, 0),
-    (4, 2, 0), (3, 6, 0), (5, 0, 0), (5, 0, 1), (4, 3, 0), (5, 1, 0), (5, 1, 1), (3, 7, 0),
-    (5, 2, 0), (5, 2, 1), (4, 4, 0), (5, 3, 0), (5, 3, 1), (4, 5, 0), (6, 1, 1), (4, 6, 0),
-    (4, 7, 0), (5, 4, 0), (5, 4, 1), (6, 3, 1), (5, 5, 0), (5, 5, 1), (5, 6, 0), (5, 6, 1),
-    (5, 7, 0), (5, 7, 1), (6, 5, 1), (6, 6, 0), (6, 7, 0),
+    (0, 0, 2), (0, 1, 2), (0, 2, 1), (0, 2, 2), (0, 0, 1), (1, 0, 0), (0, 0, 3), (1, 1, 0),
+    (0, 3, 2), (0, 5, 2), (1, 2, 0), (0, 3, 3), (0, 1, 3), (1, 3, 0), (2, 2, 1), (2, 0, 1),
+    (0, 0, 0), (0, 4, 3), (2, 0, 0), (2, 3, 0), (0, 3, 1), (0, 1, 1), (0, 4, 2), (3, 0, 0),
+    (0, 6, 3), (2, 1, 0), (2, 1, 1), (3, 1, 0), (2, 3, 1), (0, 2, 3), (0, 7, 1), (0, 5, 3),
+    (0, 2, 0), (0, 4, 0), (0, 6, 2), (2, 2, 0), (3, 2, 0), (0, 3, 0), (0, 1, 0), (1, 4, 0),
+    (0, 7, 3), (0, 6, 1), (4, 0, 0), (3, 3, 0), (0, 5, 1), (0, 7, 2), (1, 5, 0), (2, 4, 0),
+    (0, 4, 1), (4, 1, 0), (1, 7, 0), (1, 6, 0), (2, 4, 1), (4, 2, 0), (3, 4, 0), (2, 5, 0),
+    (4, 3, 0), (2, 5, 1), (5, 1, 0), (2, 7, 0), (2, 7, 1), (5, 0, 1), (3, 5, 0), (2, 6, 0),
+    (5, 1, 1), (2, 6, 1), (5, 0, 0), (5, 2, 1), (5, 2, 0), (0, 6, 0), (3, 6, 0), (4, 4, 0),
+    (5, 3, 1), (3, 7, 0), (5, 3, 0), (0, 5, 0), (0, 7, 0), (4, 5, 0), (4, 6, 0), (4, 7, 0),
+    (6, 1, 1), (5, 5, 1), (5, 4, 0), (5, 5, 0), (5, 4, 1), (5, 6, 1), (5, 6, 0), (5, 7, 1),
+    (5, 7, 0), (6, 3, 1), (6, 5, 1), (6, 6, 0), (6, 7, 0),
 )
 
 
@@ -180,13 +180,13 @@
             x2_send, x2_recv.at[g], x_sides[side],
         )
 
-    def z_near(g, side):
-        own = zbuf.at[z, slots(g)]
-        return remote(own, own, near_send, z_recv.at[g], z_sides[side])
-
-    def y_near(g, side):
-        own = ybuf.at[g, y]
-        return remote(own, own, near_send, y_recv.at[g], y_sides[side])
+    def z_near(g, side, part):
+        own = zbuf.at[z, half(g, side if part == 0 else 1 - side)]
+        return remote(own, own, near_send, (z_recv, far_recv)[part].at[g], z_sides[side])
+
+    def y_near(g, side, part):
+        own = ybuf.at[g, y, pl.ds(64 * (side if part == 0 else 1 - side), 64)]
+        return remote(own, own, near_send, (y_recv, far_recv)[part].at[g], y_sides[side])
 
     def came(at, side):
         return ((at + 1) % 4, (at + 3) % 4)[side]
@@ -236,19 +236,20 @@
         block = (mine[0, rows] + from_core[0, rows]) + (from_x2[g, 0] + from_x2[g, 1])
         zbuf[z, rows] = block
         ybuf[g, y] = block.T
-        for side in range(2):
-            z_near(g, side).start()
-            y_near(g, side).start()
+        for part in range(2):
+            for side in range(2):
+                z_near(g, side, part).start()
+                y_near(g, side, part).start()
 
     def forward(g, which):
-        arrived(from_x2.at[g], (y_recv, z_recv)[which].at[g])
+        arrived(from_x1.at[slots(g)], (y_recv, z_recv)[which].at[g])
         for side in range(2):
             (y_far, z_far)[which](g, side).start()
 
     def multiply(g, more):
         groups = (g,) if not more else (g - 1, g)
         for each in groups:
-            arrived(from_x2.at[each], far_recv.at[each])
+            arrived(from_x2.at[pl.ds(0, 2)], far_recv.at[each])
         rows = pl.ds(groups[0] * STEP, STEP * len(groups))
         right = []
         for h in range(2):
@@ -275,74 +276,106 @@
                         part = part + gram[2 * m + i, h]
                     gram[2 * m + i, h] = part
 
-    steps = (take_rows, send_x1, send_x2_early, send_x2_late, send_yz, forward, multiply)
-    for kind, group, side in ORDER:
-        steps[kind](group, side)
-
     def c1_copy(d):
         at = (x + d) % 4
         return remote(gram.at[at, 1 - k], core_gram.at[at], c1_send, c1_recv.at[d], partner)
+
+    def multiply_last(g):
+        arrived(from_x2.at[pl.ds(0, 2)], far_recv.at[g])
+        right = []
+        for h in range(2):
+            high, low = split(
+                jnp.concatenate([zbuf[2 * h, slots(g)], zbuf[2 * h + 1, slots(g)]], axis=1)
+            )
+            right.append(jnp.concatenate([high, low, high], axis=0))
+        for d in (2, 3, 1, 0):
+            at = (x + d) % 4
+            high, low = split(ybuf[g, at])
+            left = jnp.concatenate([high, high, low], axis=1)
+            for h in range(2):
+                gram[at, h] = gram[at, h] + jnp.dot(
+                    left, right[h], preferred_element_type=jnp.float32
+                )
+            c1_copy(d).start()
+
+    steps = (take_rows, send_x1, send_x2_early, send_x2_late, send_yz, forward, multiply)
+    for kind, group, side in ORDER[:-1]:
+        steps[kind](group, side)
+    multiply_last(GROUPS - 1)
 
     def combine(d):
         at = (x + d) % 4
         c1_copy(d).wait_recv()
         core_gram[at] = core_gram[at] + gram[at, k]
 
-    def c2_copy(side):
-        rows = pl.ds(64 * side, 64)
-        return remote(
-            core_gram.at[(x + 2) % 4, rows], from_c1.at[rows], c2_send, c2_recv, x_sides[side]
-        )
-
-    def c3_copy(side, late):
-        rows = pl.ds(64 * (side if late else 1 - side), 64)
+    def c_rows(side, part):
+        return pl.ds(64 * part + 32 * side, 32)
+
+    def c2_copy(side, part):
+        rows = c_rows(side, part)
+        return remote(
+            core_gram.at[(x + 2) % 4, rows], from_c1.at[rows], c2_send, c2_recv.at[part],
+            x_sides[side],
+        )
+
+    def c3_copy(side, part, late):
+        rows = c_rows(side if late else 1 - side, part)
         return remote(
             core_gram.at[(x + distances[side]) % 4, rows], from_c2.at[side, rows],
-            c3_send, c3_recv, x_sides[side],
-        )
-
-    for d in (2, 3, 1, 0):
-        c1_copy(d).start()
+            c3_send, c3_recv.at[part if late else 0], x_sides[side],
+        )
+
+    def c4_copy(j, slot, part):
+        rows = pl.ds(64 * part, 64)
+        return remote(
+            final.at[j, rows], out.at[pl.ds(pl.multiple_of(slot * 128 + 64 * part, 64), 64)],
+            c4_send.at[j], c4_recv.at[slot], owners[j],
+        )
+
+    def c4_both(j):
+        return remote(
+            final.at[j], out.at[pl.ds(j * 128, 128)], c4_send.at[j], c4_recv.at[j], owners[j]
+        )
+
+    def own_copy(j):
+        return pltpu.make_async_copy(final.at[j], out.at[pl.ds(j * 128, 128)], c4_send.at[j])
+
     combine(2)
-    for side in range(2):
-        c2_copy(side).start()
+    for part in range(2):
+        for side in range(2):
+            c2_copy(side, part).start()
     for side in range(2):
         combine(distances[side])
-        c3_copy(side, 0).start()
+        for part in range(2):
+            c3_copy(side, part, 0).start()
     combine(0)
-    arrived(from_c1, c2_recv)
-    for side in range(2):
-        at = (x + distances[side]) % 4
-        rows = pl.ds(64 * side, 64)
-        core_gram[at, rows] = core_gram[at, rows] + from_c1[rows]
-        c3_copy(side, 1).start()
+    for part in range(2):
+        arrived(from_c1.at[pl.ds(0, 64)], c2_recv.at[part])
+        for side in range(2):
+            at, rows = (x + distances[side]) % 4, c_rows(side, part)
+            core_gram[at, rows] = core_gram[at, rows] + from_c1[rows]
+            c3_copy(side, part, 1).start()
     left_here(theirs, d_send)
     left_here(mine.at[2], x1_send)
     left_here(from_x2, x2_send)
     left_here(theirs, near_send)
     left_here(from_x2, far_send)
-    arrived(from_c2, c3_recv)
-    total = (core_gram[x] + (from_c2[0] + from_c2[1])) * SCALE
-
-    def c4_copy(j, slot):
-        return remote(
-            final.at[j], out.at[pl.ds(pl.multiple_of(slot * 128, 128), 128)],
-            c4_send.at[j], c4_recv.at[slot], owners[j],
-        )
-
-    def own_copy(j):
-        return pltpu.make_async_copy(final.at[j], out.at[pl.ds(j * 128, 128)], c4_send.at[j])
-
-    for j in range(2):
-        final[j] = total[:, j * 128:(j + 1) * 128]
-    for j in range(2):
-        @pl.when(2 * k + j != z)
-        def _():
-            c4_copy(j, z % 2).start()
-
-        @pl.when(2 * k + j == z)
-        def _():
-            own_copy(j).start()
+    for part in range(2):
+        like = core_gram.at[0, pl.ds(0, 64)] if part else core_gram.at[pl.ds(0, 3), pl.ds(0, 64)]
+        arrived(like, c3_recv.at[part])
+        rows = pl.ds(64 * part, 64)
+        total = (core_gram[x, rows] + (from_c2[0, rows] + from_c2[1, rows])) * SCALE
+        for j in range(2):
+            final[j, rows] = total[:, j * 128:(j + 1) * 128]
+        for j in range(2):
+            @pl.when(2 * k + j != z)
+            def _():
+                c4_copy(j, z % 2, part).start()
+
+            if part:
+                @pl.when(2 * k + j == z)
+                def _():
+                    own_copy(j).start()
 
     left_here(core_gram, c1_send)
     left_here(from_c1, c2_send)
@@ -350,7 +383,7 @@
     for j in range(2):
         @pl.when(2 * k + j != z)
         def _():
-            c4_copy(j, j).wait()
+            c4_both(j).wait()
 
         @pl.when(2 * k + j == z)
         def _():
@@ -391,7 +424,7 @@
             vmem(2, 128, 128),
             dma((10,)), dma(()), dma((GROUPS, 4)),
             *[dma((GROUPS,))] * 5,
-            dma((4,)), dma(()), dma(()), dma((2,)), dma((2,)),
+            dma((4,)), dma((2,)), dma((2,)), dma((2,)), dma((2,)),
             *[dma(())] * 8,
         ],
         compiler_params=pltpu.CompilerParams(

time: 57.2 us -> 55 us (0.962)
  Pallas kernels: 55.6 us -> 53.3 us
    pallas_call x1, Pallas kernels: 55.6 us -> 53.3 us  [shards(): pl.pallas_call(kernel, out_shape=jax.ShapeDtypeStruct((256, 128), jnp.flo...]
where the time goes in v5:
time: 55 us; the launch traced here: 54.9 us
  Pallas kernels  53.3 us (97%)
  local copies, waits for them, and re-layouts  1.57 us (3%)
    pallas_call x1, Pallas kernels, shards(): pl.pallas_call(kernel, out_shape=jax.ShapeDtypeStruct((256, 128), jnp.flo...  53.3 us
    unnamed x1, local copies, waits for them, and re-layouts  1.57 us

profile of v5, /device:TPU:1, one launch (start us, length us, event | category | flops | bytes accessed | tf_op | source)
XLA Modules:
  0.0 54.9 jit_solution(10242537107275050697)
XLA Ops:
  0.0 53.3 %sketch.1 = f32[256,128]{1,0:T(8,128)} custom-call(s32[8192]{0:T(1024)} %samples_in.1, s32[64,128]{1,0:T(8,128)} %bitcast.1, f32[8192,128]{1,0:T(8,128)} %slab.1), custom_call_target="tpu_custom_call" | custom-call | tf_op jit(solution)/shard_map/sketch/pallas_call | solution.py:396
  53.3 1.6 %copy.5 = f32[256,128]{1,0:T(8,128)} copy(f32[256,128]{1,0:T(8,128)} %sketch.1) | data formatting | bytes 262144

commit v6 on v5

--- a/solution.py
+++ b/solution.py
@@ -19,18 +19,18 @@
 SCALE = 1.0 / (8 * SLOTS * 8 * HEIGHT)
 
 ORDER = (
-    (0, 0, 2), (0, 1, 2), (0, 2, 1), (0, 2, 2), (0, 0, 1), (1, 0, 0), (0, 0, 3), (1, 1, 0),
-    (0, 3, 2), (0, 5, 2), (1, 2, 0), (0, 3, 3), (0, 1, 3), (1, 3, 0), (2, 2, 1), (2, 0, 1),
-    (0, 0, 0), (0, 4, 3), (2, 0, 0), (2, 3, 0), (0, 3, 1), (0, 1, 1), (0, 4, 2), (3, 0, 0),
-    (0, 6, 3), (2, 1, 0), (2, 1, 1), (3, 1, 0), (2, 3, 1), (0, 2, 3), (0, 7, 1), (0, 5, 3),
-    (0, 2, 0), (0, 4, 0), (0, 6, 2), (2, 2, 0), (3, 2, 0), (0, 3, 0), (0, 1, 0), (1, 4, 0),
-    (0, 7, 3), (0, 6, 1), (4, 0, 0), (3, 3, 0), (0, 5, 1), (0, 7, 2), (1, 5, 0), (2, 4, 0),
-    (0, 4, 1), (4, 1, 0), (1, 7, 0), (1, 6, 0), (2, 4, 1), (4, 2, 0), (3, 4, 0), (2, 5, 0),
-    (4, 3, 0), (2, 5, 1), (5, 1, 0), (2, 7, 0), (2, 7, 1), (5, 0, 1), (3, 5, 0), (2, 6, 0),
-    (5, 1, 1), (2, 6, 1), (5, 0, 0), (5, 2, 1), (5, 2, 0), (0, 6, 0), (3, 6, 0), (4, 4, 0),
-    (5, 3, 1), (3, 7, 0), (5, 3, 0), (0, 5, 0), (0, 7, 0), (4, 5, 0), (4, 6, 0), (4, 7, 0),
-    (6, 1, 1), (5, 5, 1), (5, 4, 0), (5, 5, 0), (5, 4, 1), (5, 6, 1), (5, 6, 0), (5, 7, 1),
-    (5, 7, 0), (6, 3, 1), (6, 5, 1), (6, 6, 0), (6, 7, 0),
+    (0, 0, 2), (0, 1, 2), (0, 0, 1), (0, 2, 2), (0, 1, 1), (1, 0, 0), (0, 0, 3), (1, 1, 0),
+    (0, 3, 2), (0, 4, 2), (1, 2, 0), (0, 1, 3), (0, 2, 3), (1, 3, 0), (2, 0, 0), (2, 0, 1),
+    (0, 0, 0), (0, 3, 3), (2, 1, 0), (2, 1, 1), (0, 2, 1), (0, 3, 1), (0, 5, 2), (3, 0, 0),
+    (0, 4, 3), (2, 2, 0), (2, 2, 1), (3, 1, 0), (2, 3, 0), (0, 5, 3), (0, 4, 1), (0, 6, 3),
+    (0, 1, 0), (0, 2, 0), (0, 6, 2), (2, 3, 1), (3, 2, 0), (0, 3, 0), (0, 4, 0), (1, 4, 0),
+    (0, 7, 3), (0, 5, 1), (4, 0, 0), (3, 3, 0), (0, 6, 1), (0, 7, 2), (1, 5, 0), (2, 4, 0),
+    (0, 7, 1), (4, 1, 0), (1, 6, 0), (1, 7, 0), (2, 4, 1), (4, 2, 0), (3, 4, 0), (2, 5, 0),
+    (4, 3, 0), (2, 5, 1), (5, 0, 0), (2, 6, 0), (2, 6, 1), (5, 0, 1), (3, 5, 0), (2, 7, 0),
+    (5, 1, 0), (2, 7, 1), (5, 1, 1), (5, 2, 0), (5, 2, 1), (0, 5, 0), (3, 6, 0), (4, 4, 0),
+    (5, 3, 0), (3, 7, 0), (5, 3, 1), (0, 6, 0), (0, 7, 0), (4, 5, 0), (4, 6, 0), (4, 7, 0),
+    (6, 1, 1), (5, 4, 0), (5, 4, 1), (5, 5, 0), (5, 5, 1), (5, 6, 0), (5, 6, 1), (5, 7, 0),
+    (5, 7, 1), (6, 3, 1), (6, 5, 1), (6, 6, 0), (6, 7, 0),
 )
 
 
@@ -93,29 +93,27 @@
             for i in range(2)
         ]
         signed = matrix[...] * jnp.concatenate(signs, axis=1)
-        start = pl.multiple_of(q * 256, 256)
+        start = q * 256
         high, low = split(raw[pl.ds(start, 256), :])
         both = jnp.dot(
             signed, jnp.concatenate([high, low], axis=1), preferred_element_type=jnp.float32
         )
-        table[pl.ds(pl.multiple_of(q * PITCH, 8), 256), :] = both[:, :128] + both[:, 128:]
-
-    def four_inside(i, carry):
-        for u in range(4):
-            inside(4 * i + u)
-        return carry
+        table[pl.ds(q * PITCH, 256), :] = both[:, :128] + both[:, 128:]
 
     code_copy = pltpu.make_async_copy(code_rows, codes, code_sem)
     loads[0].wait()
-    for part in range(8):
-        loads[2 + part].wait()
-        four_inside(part, 0)
-        if part == 1:
+    ends = (1, 4, 8)
+    for last, end in enumerate(ends):
+        for part in range(0 if last == 0 else ends[last - 1], end):
+            loads[2 + part].wait()
+        for q in range(0 if last == 0 else 4 * ends[last - 1], 4 * end):
+            inside(q)
+        if last == 0:
             loads[1].wait()
             parity = parity_of((samples[...] // HEIGHT) & row)
             offset = samples[...] % HEIGHT
             code_rows[...] = offset + offset // 256 * (PITCH - 256) + NEGATED * parity
-        if part == 3:
+        if last == 1:
             code_copy.start()
 
     def across(t, carry):

time: 55 us -> 54.3 us (0.987)
  Pallas kernels: 53.3 us -> 52.6 us
    pallas_call x1, Pallas kernels: 53.3 us -> 52.6 us  [shards(): pl.pallas_call(kernel, out_shape=jax.ShapeDtypeStruct((256, 128), jnp.flo...]
where the time goes in v6:
time: 54.3 us; the launch traced here: 54.2 us
  Pallas kernels  52.6 us (97%)
  local copies, waits for them, and re-layouts  1.57 us (3%)
    pallas_call x1, Pallas kernels, shards(): pl.pallas_call(kernel, out_shape=jax.ShapeDtypeStruct((256, 128), jnp.flo...  52.6 us
    unnamed x1, local copies, waits for them, and re-layouts  1.57 us

profile of v6, /device:TPU:1, one launch (start us, length us, event | category | flops | bytes accessed | tf_op | source)
XLA Modules:
  0.0 54.2 jit_solution(7000112572122618813)
XLA Ops:
  0.0 52.6 %sketch.1 = f32[256,128]{1,0:T(8,128)} custom-call(s32[8192]{0:T(1024)} %samples_in.1, s32[64,128]{1,0:T(8,128)} %bitcast.1, f32[8192,128]{1,0:T(8,128)} %slab.1), custom_call_target="tpu_custom_call" | custom-call | tf_op jit(solution)/shard_map/sketch/pallas_call | solution.py:394
  52.6 1.6 %copy.5 = f32[256,128]{1,0:T(8,128)} copy(f32[256,128]{1,0:T(8,128)} %sketch.1) | data formatting | bytes 262144

commit v7 on v6

--- a/solution.py
+++ b/solution.py
@@ -12,6 +12,7 @@
 GROUPS = 8
 STEP = SLOTS // GROUPS
 HALF = STEP // 2
+PARTS = 4
 PITCH = 264
 NEGATED = HEIGHT // 256 * PITCH
 WIDE = 128
@@ -19,16 +20,16 @@
 SCALE = 1.0 / (8 * SLOTS * 8 * HEIGHT)
 
 ORDER = (
-    (0, 0, 2), (0, 1, 2), (0, 0, 1), (0, 2, 2), (0, 1, 1), (1, 0, 0), (0, 0, 3), (1, 1, 0),
-    (0, 3, 2), (0, 4, 2), (1, 2, 0), (0, 1, 3), (0, 2, 3), (1, 3, 0), (2, 0, 0), (2, 0, 1),
-    (0, 0, 0), (0, 3, 3), (2, 1, 0), (2, 1, 1), (0, 2, 1), (0, 3, 1), (0, 5, 2), (3, 0, 0),
-    (0, 4, 3), (2, 2, 0), (2, 2, 1), (3, 1, 0), (2, 3, 0), (0, 5, 3), (0, 4, 1), (0, 6, 3),
-    (0, 1, 0), (0, 2, 0), (0, 6, 2), (2, 3, 1), (3, 2, 0), (0, 3, 0), (0, 4, 0), (1, 4, 0),
-    (0, 7, 3), (0, 5, 1), (4, 0, 0), (3, 3, 0), (0, 6, 1), (0, 7, 2), (1, 5, 0), (2, 4, 0),
-    (0, 7, 1), (4, 1, 0), (1, 6, 0), (1, 7, 0), (2, 4, 1), (4, 2, 0), (3, 4, 0), (2, 5, 0),
-    (4, 3, 0), (2, 5, 1), (5, 0, 0), (2, 6, 0), (2, 6, 1), (5, 0, 1), (3, 5, 0), (2, 7, 0),
-    (5, 1, 0), (2, 7, 1), (5, 1, 1), (5, 2, 0), (5, 2, 1), (0, 5, 0), (3, 6, 0), (4, 4, 0),
-    (5, 3, 0), (3, 7, 0), (5, 3, 1), (0, 6, 0), (0, 7, 0), (4, 5, 0), (4, 6, 0), (4, 7, 0),
+    (0, 0, 2), (0, 0, 1), (0, 1, 2), (0, 2, 2), (0, 0, 3), (1, 0, 0), (0, 3, 2), (1, 1, 0),
+    (0, 4, 2), (1, 2, 0), (0, 1, 1), (0, 1, 3), (2, 0, 0), (1, 3, 0), (0, 2, 1), (0, 5, 2),
+    (0, 3, 1), (0, 2, 3), (2, 0, 1), (0, 4, 1), (0, 6, 2), (1, 4, 0), (3, 0, 0), (0, 0, 0),
+    (0, 3, 3), (2, 1, 0), (2, 1, 1), (0, 5, 1), (0, 6, 1), (0, 4, 3), (0, 1, 0), (3, 1, 0),
+    (2, 2, 0), (0, 7, 2), (0, 2, 0), (2, 2, 1), (0, 3, 0), (3, 2, 0), (2, 3, 0), (2, 3, 1),
+    (0, 5, 3), (0, 4, 0), (3, 3, 0), (4, 0, 0), (1, 5, 0), (0, 5, 0), (0, 6, 3), (0, 7, 1),
+    (4, 1, 0), (1, 6, 0), (0, 6, 0), (2, 4, 0), (2, 4, 1), (3, 4, 0), (1, 7, 0), (4, 2, 0),
+    (2, 5, 0), (4, 3, 0), (0, 7, 3), (2, 5, 1), (5, 0, 0), (3, 5, 0), (2, 6, 0), (5, 0, 1),
+    (2, 6, 1), (3, 6, 0), (2, 7, 0), (2, 7, 1), (5, 1, 0), (5, 1, 1), (5, 2, 0), (5, 2, 1),
+    (4, 4, 0), (0, 7, 0), (3, 7, 0), (5, 3, 0), (5, 3, 1), (4, 5, 0), (4, 6, 0), (4, 7, 0),
     (6, 1, 1), (5, 4, 0), (5, 4, 1), (5, 5, 0), (5, 5, 1), (5, 6, 0), (5, 6, 1), (5, 7, 0),
     (5, 7, 1), (6, 3, 1), (6, 5, 1), (6, 6, 0), (6, 7, 0),
 )
@@ -307,7 +308,7 @@
         core_gram[at] = core_gram[at] + gram[at, k]
 
     def c_rows(side, part):
-        return pl.ds(64 * part + 32 * side, 32)
+        return pl.ds(128 // PARTS * part + 64 // PARTS * side, 64 // PARTS)
 
     def c2_copy(side, part):
         rows = c_rows(side, part)
@@ -324,9 +325,9 @@
         )
 
     def c4_copy(j, slot, part):
-        rows = pl.ds(64 * part, 64)
-        return remote(
-            final.at[j, rows], out.at[pl.ds(pl.multiple_of(slot * 128 + 64 * part, 64), 64)],
+        rows = pl.ds(128 // PARTS * part, 128 // PARTS)
+        return remote(
+            final.at[j, rows], out.at[pl.ds(pl.multiple_of(slot * 128 + 128 // PARTS * part, 8), 128 // PARTS)],
             c4_send.at[j], c4_recv.at[slot], owners[j],
         )
 
@@ -339,16 +340,16 @@
         return pltpu.make_async_copy(final.at[j], out.at[pl.ds(j * 128, 128)], c4_send.at[j])
 
     combine(2)
-    for part in range(2):
+    for part in range(PARTS):
         for side in range(2):
             c2_copy(side, part).start()
     for side in range(2):
         combine(distances[side])
-        for part in range(2):
+        for part in range(PARTS):
             c3_copy(side, part, 0).start()
     combine(0)
-    for part in range(2):
-        arrived(from_c1.at[pl.ds(0, 64)], c2_recv.at[part])
+    for part in range(PARTS):
+        arrived(from_c1.at[pl.ds(0, 128 // PARTS)], c2_recv.at[part])
         for side in range(2):
             at, rows = (x + distances[side]) % 4, c_rows(side, part)
             core_gram[at, rows] = core_gram[at, rows] + from_c1[rows]
@@ -358,10 +359,10 @@
     left_here(from_x2, x2_send)
     left_here(theirs, near_send)
     left_here(from_x2, far_send)
-    for part in range(2):
-        like = core_gram.at[0, pl.ds(0, 64)] if part else core_gram.at[pl.ds(0, 3), pl.ds(0, 64)]
-        arrived(like, c3_recv.at[part])
-        rows = pl.ds(64 * part, 64)
+    for part in range(PARTS):
+        size = 256 // PARTS + (256 if part == 0 else 0)
+        arrived(from_core.at[0, pl.ds(0, size)], c3_recv.at[part])
+        rows = pl.ds(128 // PARTS * part, 128 // PARTS)
         total = (core_gram[x, rows] + (from_c2[0, rows] + from_c2[1, rows])) * SCALE
         for j in range(2):
             final[j, rows] = total[:, j * 128:(j + 1) * 128]
@@ -370,7 +371,7 @@
             def _():
                 c4_copy(j, z % 2, part).start()
 
-            if part:
+            if part == PARTS - 1:
                 @pl.when(2 * k + j == z)
                 def _():
                     own_copy(j).start()
@@ -422,7 +423,7 @@
             vmem(2, 128, 128),
             dma((10,)), dma(()), dma((GROUPS, 4)),
             *[dma((GROUPS,))] * 5,
-            dma((4,)), dma((2,)), dma((2,)), dma((2,)), dma((2,)),
+            dma((4,)), dma((PARTS,)), dma((PARTS,)), dma((2,)), dma((2,)),
             *[dma(())] * 8,
         ],
         compiler_params=pltpu.CompilerParams(

time: 54.3 us -> 53.9 us (level)
  no operation moved by 1% of the time
where the time goes in v7:
time: 53.9 us; the launch traced here: 53.7 us
  Pallas kernels  52.2 us (97%)
  local copies, waits for them, and re-layouts  1.57 us (3%)
    pallas_call x1, Pallas kernels, shards(): pl.pallas_call(kernel, out_shape=jax.ShapeDtypeStruct((256, 128), jnp.flo...  52.2 us
    unnamed x1, local copies, waits for them, and re-layouts  1.57 us

profile of v7, /device:TPU:1, one launch (start us, length us, event | category | flops | bytes accessed | tf_op | source)
XLA Modules:
  0.0 53.7 jit_solution(15039021200184508920)
XLA Ops:
  0.0 52.2 %sketch.1 = f32[256,128]{1,0:T(8,128)} custom-call(s32[8192]{0:T(1024)} %samples_in.1, s32[64,128]{1,0:T(8,128)} %bitcast.1, f32[8192,128]{1,0:T(8,128)} %slab.1), custom_call_target="tpu_custom_call" | custom-call | tf_op jit(solution)/shard_map/sketch/pallas_call | solution.py:395
  52.2 1.6 %copy.5 = f32[256,128]{1,0:T(8,128)} copy(f32[256,128]{1,0:T(8,128)} %sketch.1) | data formatting | bytes 262144

commit v8 on v7

--- a/solution.py
+++ b/solution.py
@@ -12,7 +12,7 @@
 GROUPS = 8
 STEP = SLOTS // GROUPS
 HALF = STEP // 2
-PARTS = 4
+PARTS = 8
 PITCH = 264
 NEGATED = HEIGHT // 256 * PITCH
 WIDE = 128

time: 53.9 us -> 53.7 us (level)
  no operation moved by 1% of the time
where the time goes in v8:
time: 53.7 us; the launch traced here: 53.6 us
  Pallas kernels  52 us (97%)
  local copies, waits for them, and re-layouts  1.57 us (3%)
    pallas_call x1, Pallas kernels, shards(): pl.pallas_call(kernel, out_shape=jax.ShapeDtypeStruct((256, 128), jnp.flo...  52 us
    unnamed x1, local copies, waits for them, and re-layouts  1.57 us

profile of v8, /device:TPU:1, one launch (start us, length us, event | category | flops | bytes accessed | tf_op | source)
XLA Modules:
  0.0 53.6 jit_solution(10939069632035578176)
XLA Ops:
  0.0 52.0 %sketch.1 = f32[256,128]{1,0:T(8,128)} custom-call(s32[8192]{0:T(1024)} %samples_in.1, s32[64,128]{1,0:T(8,128)} %bitcast.1, f32[8192,128]{1,0:T(8,128)} %slab.1), custom_call_target="tpu_custom_call" | custom-call | tf_op jit(solution)/shard_map/sketch/pallas_call | solution.py:395
  52.0 1.6 %copy.5 = f32[256,128]{1,0:T(8,128)} copy(f32[256,128]{1,0:T(8,128)} %sketch.1) | data formatting | bytes 262144
